TPU v7x, 256 devices: a whole 4x4x8 slice. The times are simulated.
256 devices in a mesh: dp: 16 (over x, y), seq: 16 (over z, core).
Axes of the slice: x: 4, y: 4, z: 8, core: 2. Of those that a mesh axis runs over, the one named last changes fastest.
Arguments:
- tokens: bfloat16 [16, 2048, 5120], P('dp', 'seq'), may hold values from -6 to 6
- base_query: bfloat16 [16, 2048, 2560], P('dp', 'seq'), may hold values from -96 to 96
- k_base: bfloat16 [16, 2048, 2560], P('dp', 'seq'), may hold values from -4 to 4
- v_base: bfloat16 [16, 2048, 2560], P('dp', 'seq'), may hold values from -6 to 6
- cotangent: bfloat16 [16, 2048, 2560], P('dp', 'seq'), may hold values from -0.0066223145 to 0.0066223145
- adapter_down: bfloat16 [5120, 256], replicated, may hold values from -0.078125 to 0.078125
- adapter_up_weight: bfloat16 [256, 2560], replicated, may hold values from -1 to 1
- gate_weight: bfloat16 [8, 5120], replicated, may hold values from -0.078125 to 0.078125
Outputs:
- attended: bfloat16 [16, 2048, 2560], P('dp', 'seq')
- gate_grad: float32 [8, 5120], replicated
All inputs are finite; a program needn't handle non-finite values.
Results may differ from a plain program's by a relative error of at most 0.03.
Values may be sent and summed in bfloat16 or wider, within the bound.
No kernel may reach another device: no remote copies, remote signals or barrier semaphores. Data moves between devices by JAX's collectives and lax.ppermute only.
A program may use at most 192 MiB of HBM per device.

v0:
```python
import functools
import math

import jax
import jax.numpy as jnp
from jax import lax
from jax.experimental import pallas as pl
from jax.experimental.pallas import tpu as pltpu
from jax.sharding import Mesh
from jax.sharding import PartitionSpec as P


HEAD_DIM = 128
EXPERTS = 8
RANK = 32
CORES = 2
AXES = ("x", "y", "z", "c")
SEQ = ("z", "c")
DP = ("x", "y")
ADAPTER_SCALE = 2.0
SCORE_SCALE = HEAD_DIM ** (-0.5)
EXP2_SCALE = SCORE_SCALE * math.log2(math.e)
MASKED = -1e30

bf16, f32 = jnp.bfloat16, jnp.float32
WHOLE = pl.BlockSpec(memory_space=pltpu.VMEM)
SCALAR = pl.BlockSpec(memory_space=pltpu.SMEM)
VMEM_LIMIT = 20 * 1024 * 1024


def rows_dot(a, b, precision=None):
    return lax.dot_general(
        a, b, (((1,), (1,)), ((), ())), precision=precision, preferred_element_type=f32
    )


def pack_body(a, b, mine, other, held, came, went):
    half = a.shape[2] // CORES
    core = lax.axis_index("c")
    pairs = []
    for i, (out, which) in enumerate(((mine, core), (other, 1 - core))):
        for j, source in enumerate((a, b)):
            n = len(pairs)
            columns = pl.ds(pl.multiple_of(which * half, HEAD_DIM), half)
            at = pl.ds(j * half, half)
            pairs.append(
                (
                    pltpu.make_async_copy(source.at[0, :, columns], held.at[i, :, at], came.at[n]),
                    pltpu.make_async_copy(held.at[i, :, at], out.at[:, at], went.at[n]),
                )
            )
    for come, _ in pairs:
        come.start()
    for come, go in pairs:
        come.wait()
        go.start()
    for _, go in pairs:
        go.wait()


def pack(a, b):
    _, rows, width = a.shape
    return pl.pallas_call(
        pack_body,
        in_specs=[pl.BlockSpec(memory_space=pl.ANY)] * 2,
        out_specs=[pl.BlockSpec(memory_space=pl.ANY)] * 2,
        out_shape=[pltpu.HBM((rows, width), a.dtype)] * 2,
        scratch_shapes=[
            pltpu.VMEM((CORES, rows, width), a.dtype),
            pltpu.SemaphoreType.DMA((2 * CORES,)),
            pltpu.SemaphoreType.DMA((2 * CORES,)),
        ],
        name="pack",
        cost_estimate=pl.CostEstimate(flops=2_000_000, bytes_accessed=5_000_000, transcendentals=0),
    )(a, b)


def expert_columns(columns):
    e = lax.broadcasted_iota(jnp.int32, (EXPERTS, columns), 0)
    col = lax.broadcasted_iota(jnp.int32, (EXPERTS, columns), 1)
    return (col // RANK == e).astype(f32)


def query_body(tok_mine, tok_other, down, gate, up, mine, other, query, low_out, gates_out):
    rows = tok_mine.shape[0]
    half = up.shape[1]
    spread = expert_columns(down.shape[1])
    for part, tok, base in ((0, tok_mine, mine), (1, tok_other, other)):
        at = slice(part * rows, (part + 1) * rows)
        t = tok[...]
        logits = rows_dot(t, gate[...])
        e = jnp.exp(logits - jnp.max(logits, axis=-1, keepdims=True))
        gates = e / jnp.sum(e, axis=-1, keepdims=True)
        low = jnp.dot(t, down[...], preferred_element_type=f32).astype(bf16)
        wide = jnp.dot(gates, spread, precision=lax.Precision.HIGHEST, preferred_element_type=f32)
        mixed = (low.astype(f32) * wide).astype(bf16)
        product = jnp.dot(mixed, up[...], preferred_element_type=f32)
        query[at, :] = (base[:, :half].astype(f32) + ADAPTER_SCALE * product).astype(bf16)
        low_out[at, :] = low
        gates_out[:, at] = gates.T


def make_query(tok_mine, tok_other, down, gate, up_half, mine, other):
    rows = tok_mine.shape[0] * CORES
    half = up_half.shape[1]
    return pl.pallas_call(
        query_body,
        in_specs=[WHOLE] * 7,
        out_specs=[WHOLE] * 3,
        out_shape=[
            jax.ShapeDtypeStruct((rows, half), bf16),
            jax.ShapeDtypeStruct((rows, down.shape[1]), bf16),
            jax.ShapeDtypeStruct((EXPERTS, rows), f32),
        ],
        name="query",
        compiler_params=pltpu.CompilerParams(vmem_limit_bytes=VMEM_LIMIT),
        cost_estimate=pl.CostEstimate(
            flops=2 * rows * 256 * (5120 + half), bytes_accessed=8_000_000, transcendentals=0
        ),
    )(tok_mine, tok_other, down, gate, up_half, mine, other)


def tiled(x, width):
    return jnp.concatenate([x] * (width // x.shape[1]), axis=1)


def step(q, cot, keys, values, state, mask):
    wide = (q.shape[0], HEAD_DIM)
    scores = rows_dot(q, keys)
    if mask is not None:
        scores = jnp.where(mask, scores, MASKED)
    top = jnp.broadcast_to(jnp.max(scores, axis=-1, keepdims=True), wide)
    if state is not None:
        top = jnp.maximum(top, state[0])
        fade = jnp.exp2((state[0] - top) * EXP2_SCALE)
    weights = jnp.exp2((scores - tiled(top, scores.shape[1])) * EXP2_SCALE)
    products = weights * rows_dot(cot, values)
    total = jnp.broadcast_to(jnp.sum(weights, axis=-1, keepdims=True), wide)
    delta = jnp.broadcast_to(jnp.sum(products, axis=-1, keepdims=True), wide)
    both = jnp.dot(
        weights.astype(bf16), jnp.concatenate([values, keys], axis=1), preferred_element_type=f32
    )
    acc_v, acc_k = both[:, :HEAD_DIM], both[:, HEAD_DIM:]
    acc_g = jnp.dot(products.astype(bf16), keys, preferred_element_type=f32)
    if state is not None:
        total = total + fade * state[1]
        delta = delta + fade * state[2]
        acc_v = acc_v + fade * state[3]
        acc_k = acc_k + fade * state[4]
        acc_g = acc_g + fade * state[5]
    return top, total, delta, acc_v, acc_k, acc_g


STATES = 6


def attend_body(*refs, kind, reach, heads, first=0):
    refs = list(refs)
    place, _, query, cot_mine, other = refs[:5]
    del refs[:5]
    count = {"own": 2, "far": 4, "edge": 2, "close": 2}[kind]
    pieces = refs[:count]
    del refs[:count]
    state_in = None
    if kind != "own":
        state_in = refs[:STATES]
        del refs[:STATES]
    half = cot_mine.shape[1]
    rows = cot_mine.shape[0]
    both_rows = CORES * rows
    core, z = place[0], place[1]
    unroll = 2 if heads % 2 == 0 else heads

    def columns(h, base=0):
        return pl.ds(pl.multiple_of(h * HEAD_DIM + base, HEAD_DIM), HEAD_DIM)

    def head(h, piece_refs, mask=None):
        at = columns(h + first)
        cot = jnp.concatenate([cot_mine[:, at], other[:, columns(h + first, half)]], axis=0)
        keys = jnp.concatenate([p[:, columns(h)] for p in piece_refs], axis=0)
        values_at = columns(h, heads * HEAD_DIM)
        values = jnp.concatenate([p[:, values_at] for p in piece_refs], axis=0)
        state = None if state_in is None else tuple(s[:, at] for s in state_in)
        return step(query[:, at], cot, keys, values, state, mask)

    if kind in ("own", "far"):
        token_out, state_out = refs[0], refs[1:]
        token_out[...] = jnp.zeros_like(token_out)

        def run(piece_refs, mask=None):
            def one_head(h, carry):
                new = head(h, piece_refs, mask)
                for ref, value in zip(state_out, new, strict=True):
                    ref[:, columns(h)] = value
                return carry

            lax.fori_loop(0, heads, one_head, 0, unroll=unroll)

        if kind == "own":
            shape = (both_rows, both_rows)
            r = lax.broadcasted_iota(jnp.int32, shape, 0)
            s = lax.broadcasted_iota(jnp.int32, shape, 1)
            mine_at, other_at = core * rows, (1 - core) * rows - rows
            row_at = r + jnp.where(r < rows, mine_at, other_at)
            key_at = s + jnp.where(s < rows, mine_at, other_at)
            run(pieces, key_at <= row_at)
            return
        near, wrapped = reach

        @pl.when(z >= wrapped)
        def _():
            run(pieces)

        @pl.when(jnp.logical_and(z >= near, z < wrapped))
        def _():
            run(pieces[:2])

        @pl.when(z < near)
        def _():
            for a, b in zip(state_in, state_out, strict=True):
                b[...] = a[...]

        return

    if kind == "close":
        early, up, low, gates, tok_mine, tok_other = refs[:6]
        del refs[:6]
        att_mine, att_other, grad, dqueries, att, sems = refs
    else:
        att_mine, att_other, dqueries, att, sems = refs

    def outs(at):
        return [
            pltpu.make_async_copy(att.at[pl.ds(0, rows), at], att_mine.at[:, at], sems.at[0]),
            pltpu.make_async_copy(att.at[pl.ds(rows, rows), at], att_other.at[:, at], sems.at[1]),
        ]

    def close(seen):
        def one_head(h, carry):
            at = columns(h)
            state = head(h, pieces) if seen else tuple(s[:, columns(h + first)] for s in state_in)
            _, total, delta, acc_v, acc_k, acc_g = state
            inverse = 1.0 / total
            att[:, at] = (acc_v * inverse).astype(bf16)
            for copy in outs(at):
                copy.start()
            dquery = SCORE_SCALE * (acc_g * inverse - (delta * inverse) * (acc_k * inverse))
            dqueries[:, at] = dquery.astype(bf16)
            return carry

        lax.fori_loop(0, heads, one_head, 0, unroll=unroll)

    seen = z >= reach[0]
    pl.when(seen)(lambda: close(True))
    pl.when(jnp.logical_not(seen))(lambda: close(False))
    if kind == "edge":
        for copy in outs(pl.ds(0, heads * HEAD_DIM)):
            copy.wait()
        return
    split = first * HEAD_DIM
    spread = expert_columns(up.shape[0]).astype(bf16)
    dmixed = rows_dot(early[...], up[:, :split]) + rows_dot(dqueries[...], up[:, split:])
    product = ADAPTER_SCALE * dmixed * low[...].astype(f32)
    dgates = jnp.zeros((EXPERTS, both_rows), f32)
    for _ in range(3):
        part = product.astype(bf16)
        dgates = dgates + rows_dot(spread, part)
        product = product - part.astype(f32)
    g = gates[...]
    dlogits = (g * (dgates - jnp.sum(g * dgates, axis=0, keepdims=True))).astype(bf16)
    width = tok_mine.shape[1]
    chunk = CORES * LANES
    total = jnp.concatenate(
        [
            jnp.dot(
                dlogits,
                jnp.concatenate([tok_mine[:, at : at + chunk], tok_other[:, at : at + chunk]], axis=0),
                preferred_element_type=f32,
            )
            for at in range(0, width, chunk)
        ],
        axis=1,
    )
    per_block = grad.shape[1] // HALF_TILE
    for i in range(grad.shape[0] * per_block):
        t, u = i // 2, i % 2
        b, j = i // per_block, i % per_block
        grad[b, j * HALF_TILE : (j + 1) * HALF_TILE, :] = total[
            u * HALF_TILE : (u + 1) * HALF_TILE, t * LANES : (t + 1) * LANES
        ].astype(bf16)
    for copy in outs(pl.ds(0, heads * HEAD_DIM)):
        copy.wait()


HALF_TILE = EXPERTS // 2
LANES = 128


def gather_blocks_body(blocks, out):
    per_block = blocks.shape[1] // HALF_TILE
    for i in range(blocks.shape[0] * per_block):
        t, u = i // 2, i % 2
        b, j = i // per_block, i % per_block
        out[u * HALF_TILE : (u + 1) * HALF_TILE, t * LANES : (t + 1) * LANES] = blocks[
            b, j * HALF_TILE : (j + 1) * HALF_TILE, :
        ].astype(f32)


def in_vmem(x):
    return pltpu.with_memory_space_constraint(x, pltpu.VMEM)


def attend(kind, reach, place, token, query, cot_mine, other, pieces, state, tail=()):
    both_rows, half = query.shape
    heads = pieces[0].shape[1] // (2 * HEAD_DIM)
    rows = both_rows // CORES
    here = heads * HEAD_DIM
    first = 0
    operands = [place, token, query, cot_mine, other, *pieces, *state, *tail]
    if kind in ("own", "far"):
        out_shape = [jax.ShapeDtypeStruct((8, LANES), f32)]
        out_shape += [pltpu.VMEM((both_rows, half), f32)] * STATES
        out_specs = [WHOLE] * len(out_shape)
        scratch = []
    else:
        out_shape = [pltpu.HBM((rows, here), bf16)] * CORES
        scratch = [pltpu.VMEM((both_rows, here), bf16), pltpu.SemaphoreType.DMA((CORES,))]
        if kind == "edge":
            out_shape += [pltpu.VMEM((both_rows, here), bf16)]
        else:
            first = tail[0].shape[1] // HEAD_DIM
            n, width = lax.axis_size(SEQ), tail[-1].shape[1]
            blocks = (n, EXPERTS * width // n // LANES, LANES)
            out_shape += [jax.ShapeDtypeStruct(blocks, bf16)]
            scratch = [pltpu.VMEM((both_rows, here), bf16)] + scratch
        out_specs = [pl.BlockSpec(memory_space=pl.ANY)] * CORES + [WHOLE]
    keys = sum(p.shape[0] for p in pieces)
    return pl.pallas_call(
        functools.partial(attend_body, kind=kind, reach=reach, heads=heads, first=first),
        in_specs=[SCALAR, pl.BlockSpec(memory_space=pl.ANY)] + [WHOLE] * (len(operands) - 2),
        out_specs=out_specs,
        out_shape=out_shape,
        scratch_shapes=scratch,
        compiler_params=pltpu.CompilerParams(vmem_limit_bytes=VMEM_LIMIT),
        cost_estimate=pl.CostEstimate(
            flops=20 * both_rows * keys * here, bytes_accessed=8_000_000, transcendentals=0
        ),
    )(*operands)


def sent(value, axis, size):
    copies = jnp.broadcast_to(value[None], (size, *value.shape))
    return lax.all_to_all(copies, axis, 0, 0, tiled=True)


def total_of(blocks, shape):
    own = lax.all_to_all(blocks, SEQ, 0, 0, tiled=True).astype(f32).sum(axis=0).astype(bf16)
    own = sent(own, DP, lax.axis_size(DP)).astype(f32).sum(axis=0).astype(bf16)
    whole = in_vmem(sent(own, SEQ, lax.axis_size(SEQ)))
    return pl.pallas_call(
        gather_blocks_body,
        in_specs=[WHOLE],
        out_specs=WHOLE,
        out_shape=jax.ShapeDtypeStruct(shape, f32),
        name="gather_blocks",
    )(whole)


def after(arrays, token):
    *arrays, token = lax.optimization_barrier((*arrays, token))
    return arrays, token


def shards(tokens, base_query, k_base, v_base, cotangent, adapter_down, up_weight, gate_weight):
    width = k_base.shape[2]
    half = width // CORES
    n = lax.axis_size("z")
    core, z = lax.axis_index("c"), lax.axis_index("z")
    place = jnp.stack([core, z]).astype(jnp.int32)
    ahead = [(i, (i + 1) % n) for i in range(n)]
    back = [(i, (i - 1) % n) for i in range(n)]
    swap = [(0, 1), (1, 0)]

    def cross(way):
        return [(2 * i + c, 2 * ((i + way) % n) + 1 - c) for i in range(n) for c in range(2)]

    a0, other_kv = pack(k_base, v_base)
    fa = [a0, lax.ppermute(a0, "z", ahead)]
    kb = [None, lax.ppermute(other_kv, SEQ, cross(-1))]
    b0 = lax.ppermute(other_kv, "c", swap)
    fb = [b0, lax.ppermute(other_kv, SEQ, cross(1))]
    ka = [a0, lax.ppermute(a0, "z", back)]
    mine_qc, other_qc = pack(base_query, cotangent)
    qc = lax.ppermute(other_qc, "c", swap)
    tok_mine = tokens[0]
    tok_other = lax.ppermute(tok_mine, "c", swap)

    up_half = lax.dynamic_slice_in_dim(up_weight, core * half, half, 1)
    query, low, gates = make_query(
        tok_mine, tok_other, adapter_down, gate_weight, up_half, mine_qc, qc
    )
    cot_mine = mine_qc[:, half:]
    common = (query, cot_mine, qc)
    fa.append(lax.ppermute(fa[1], "z", ahead))
    kb.append(lax.ppermute(kb[1], "z", back))
    token = jnp.zeros((8, LANES), f32)
    token, *state = attend("own", None, place, token, *common, (a0, b0), ())
    (x, y), token = after((fb[1], ka[1]), token)
    fb.append(lax.ppermute(x, "z", ahead))
    ka.append(lax.ppermute(y, "z", back))
    for d in range(1, n // 2):
        pieces = (fa[d], fb[d], ka[d], kb[d])
        state = [in_vmem(s) for s in state]
        token, *state = attend("far", (d, n - d), place, token, *common, pieces, state)
        if d + 1 < n // 2:
            (x, y), token = after((fa[d + 1], kb[d + 1]), token)
            if d + 2 < n // 2:
                fa.append(lax.ppermute(x, "z", ahead))
                kb.append(lax.ppermute(y, "z", back))
        if d + 2 < n // 2:
            fb.append(moved(fb[d + 1], ahead))
            ka.append(moved(ka[d + 1], back))
    parts = []
    for j in range(2):
        cut = [head_part(p, j) for p in (x, y)]
        parts.append((moved(cut[0], ahead), moved(cut[1], back)))
    common = tuple(in_vmem(v) for v in common)
    state = [in_vmem(v) for v in state]
    reach = (n // 2, n)
    mine_1, other_1, early = attend("edge", reach, place, token, *common, parts[0], state)
    tail = (in_vmem(early), in_vmem(up_half), low, gates, in_vmem(tok_mine), in_vmem(tok_other))
    mine_2, other_2, grad = attend("close", reach, place, token, *common, parts[1], state, tail)
    back_1, back_2 = lax.ppermute(other_1, "c", swap), lax.ppermute(other_2, "c", swap)
    attended = jnp.where(
        core == 0,
        jnp.concatenate([mine_1, mine_2, back_1, back_2], axis=1),
        jnp.concatenate([back_1, back_2, mine_1, mine_2], axis=1),
    )
    return attended[None], total_of(grad, (EXPERTS, tokens.shape[2]))


def moved(value, pairs):
    return lax.ppermute(value, "z", pairs)


def head_part(piece, j):
    width = piece.shape[1] // 4
    keys = piece[:, j * width : (j + 1) * width]
    values = piece[:, (2 + j) * width : (3 + j) * width]
    return jnp.concatenate([keys, values], axis=1)


def solution(mesh):
    split = Mesh(mesh.devices.reshape(4, 4, 8, 2), AXES)
    rows = P(DP, SEQ, None)
    return jax.shard_map(
        shards,
        mesh=split,
        in_specs=(rows,) * 5 + (P(),) * 3,
        out_specs=(rows, P()),
        check_vma=False,
    )
```

profile of v0, /device:TPU:1, one launch (start us, length us, event | category | flops | bytes accessed | tf_op | source)
XLA Modules:
  0.0 168.4 jit_solution(14633513060330249210)
XLA Ops:
  0.6 3.3 %collective-permute-start.6 = (bf16[128,5120]{1,0:T(8,128)(2,1)}, bf16[128,5120]{1,0:T(8,128)(2,1)}, u32[]{:S(2)}, u32[]{:S(2)}) collective-permute-start(bf16[128,5120]{1,0:T(8,128)(2,1)} %bitcast.7), channel_id=1, source_target_pairs={{0,1},{1,0},{2,3},{3,2},{4,5},{5,4},{6,7},{7,6},{8,9},{9,8},{10,11... | collective-permute-start | bytes 3932168 | tf_op jit(solution)/shard_map/ppermute | solution.py:396
  8.5 4.2 %collective-permute-start.2 = (bf16[128,2560]{1,0:T(8,128)(2,1)}, bf16[128,2560]{1,0:T(8,128)(2,1)}, u32[]{:S(2)}, u32[]{:S(2)}) collective-permute-start(bf16[128,2560]{1,0:T(8,128)(2,1)} %get-tuple-element.53), channel_id=1, source_target_pairs={{0,15},{1,14},{2,1},{3,0},{4,3},{5,2},{6,5},{7,4},{8,7},{9,6},{10,... | collective-permute-start | bytes 1966088 | tf_op jit(solution)/shard_map/ppermute | solution.py:389
  12.9 14.5 %collective-permute-done.refs_5_ = bf16[128,2560]{1,0:T(8,128)(2,1)} collective-permute-done((bf16[128,2560]{1,0:T(8,128)(2,1)}, bf16[128,2560]{1,0:T(8,128)(2,1)}, u32[]{:S(2)}, u32[]{:S(2)}) %collective-permute-start) | collective-permute-done | bytes 655392 | tf_op jit(solution)/shard_map/ppermute | solution.py:388
  30.7 2.4 %collective-permute-start.3 = (bf16[128,2560]{1,0:T(8,128)(2,1)}, bf16[128,2560]{1,0:T(8,128)(2,1)S(1)}, u32[]{:S(2)}, u32[]{:S(2)}) collective-permute-start(bf16[128,2560]{1,0:T(8,128)(2,1)} %collective-permute-done.2.refs_8_), channel_id=1, source_target_pairs={{0,14},{2,0},{4,2},{6,4},{8,6},{10,8},{12,10},{14,12},{1,15},{3,1}... | collective-permute-start | bytes 1966088 | tf_op jit(solution)/shard_map/ppermute | solution.py:405
  35.0 4.3 %query.1 = (bf16[256,1280]{1,0:T(8,128)(2,1)S(1)}, bf16[256,256]{1,0:T(8,128)(2,1)S(1)}, f32[8,256]{1,0:T(8,128)S(1)}) custom-call(bf16[128,5120]{1,0:T(8,128)(2,1)S(1)} %bitcast.8, bf16[128,5120]{1,0:T(8,128)(2,1)} %collective-permute-done.6.tok_other.refs_18_, bf16[5120,256]{1,0:T(8,128)(2,1)S(1)} %copy-done.3, bf16[8,5120]{1,0:T(8,128)(2,1)S(1)} %copy-done.5, ...), custom_call_target="tpu_custom_call" | custom-call | flops 838860800 | bytes 8000000 | tf_op jit(solution)/shard_map/query/pallas_call | solution.py:106
  39.3 4.9 %shard_map.95 = (f32[8,128]{1,0:T(8,128)S(1)}, f32[256,1280]{1,0:T(8,128)S(1)}, f32[256,1280]{1,0:T(8,128)S(1)}, f32[256,1280]{1,0:T(8,128)S(1)}, f32[256,1280]{...) custom-call(s32[2]{0:T(128)S(1)} %pad_add_fusion.refs_0_, f32[8,128]{1,0:T(8,128)S(1)} %broadcast_in_dim.6.refs_1_, ...), custom_call_target="tpu_custom_call" | custom-call | flops 1677721600 | bytes 8000000 | tf_op jit(solution)/shard_map/pallas_call | solution.py:338
  44.3 2.7 %collective-permute-start.12 = (bf16[128,2560]{1,0:T(8,128)(2,1)}, bf16[128,2560]{1,0:T(8,128)(2,1)S(1)}, u32[]{:S(2)}, u32[]{:S(2)}) collective-permute-start(bf16[128,2560]{1,0:T(8,128)(2,1)} %collective-permute-done.5.refs_7_), channel_id=1, source_target_pairs={{0,14},{2,0},{4,2},{6,4},{8,6},{10,8},{12,10},{14,12},{1,15},{3,1}... | collective-permute-start | bytes 1966088 | tf_op jit(solution)/shard_map/ppermute | solution.py:410
  47.0 2.4 %shard_map.96 = (f32[8,128]{1,0:T(8,128)S(1)}, f32[256,1280]{1,0:T(8,128)S(1)}, f32[256,1280]{1,0:T(8,128)S(1)}, f32[256,1280]{1,0:T(8,128)S(1)}, f32[256,1280]{...) custom-call(s32[2]{0:T(128)S(1)} %pad_add_fusion.refs_0_, f32[8,128]{1,0:T(8,128)S(1)} %get-tuple-element.58.refs_1_, ...), custom_call_target="tpu_custom_call" | custom-call | flops 3355443200 | bytes 8000000 | tf_op jit(solution)/shard_map/pallas_call | solution.py:338
  49.4 6.0 %collective-permute-done.1.refs_5_ = bf16[128,2560]{1,0:T(8,128)(2,1)S(1)} collective-permute-done((bf16[128,2560]{1,0:T(8,128)(2,1)}, bf16[128,2560]{1,0:T(8,128)(2,1)S(1)}, u32[]{:S(2)}, u32[]{:S(2)}) %collective-permute-start.1) | collective-permute-done | bytes 655392 | tf_op jit(solution)/shard_map/ppermute | solution.py:404
  58.2 11.2 %collective-permute-done.11.refs_6_ = bf16[128,2560]{1,0:T(8,128)(2,1)S(1)} collective-permute-done((bf16[128,2560]{1,0:T(8,128)(2,1)}, bf16[128,2560]{1,0:T(8,128)(2,1)S(1)}, u32[]{:S(2)}, u32[]{:S(2)}) %collective-permute-start.11) | collective-permute-done | bytes 655392 | tf_op jit(solution)/shard_map/ppermute | solution.py:409
  71.5 13.0 %collective-permute-done.10.refs_8_ = bf16[128,2560]{1,0:T(8,128)(2,1)S(1)} collective-permute-done((bf16[128,2560]{1,0:T(8,128)(2,1)S(1)}, bf16[128,2560]{1,0:T(8,128)(2,1)S(1)}, u32[]{:S(2)}, u32[]{:S(2)}) %collective-permute-start.10) | collective-permute-done | bytes 655392 | tf_op jit(solution)/shard_map/ppermute | solution.py:419
  86.6 2.7 %collective-permute-start.14 = (bf16[128,2560]{1,0:T(8,128)(2,1)S(1)}, bf16[128,2560]{1,0:T(8,128)(2,1)S(1)}, u32[]{:S(2)}, u32[]{:S(2)}) collective-permute-start(bf16[128,2560]{1,0:T(8,128)(2,1)S(1)} %collective-permute-done.12.refs_7_), channel_id=1, source_target_pairs={{0,14},{2,0},{4,2},{6,4},{8,6},{10,8},{12,10},{14,12},{1,15},{3,1}... | collective-permute-start | bytes 1966088 | tf_op jit(solution)/shard_map/ppermute | solution.py:443
  89.4 2.7 %collective-permute-start.18 = (bf16[128,1280]{1,0:T(8,128)(2,1)S(1)}, bf16[128,1280]{1,0:T(8,128)(2,1)S(1)}, u32[]{:S(2)}, u32[]{:S(2)}) collective-permute-start(bf16[128,1280]{1,0:T(8,128)(2,1)S(1)} %pad_maximum_fusion.3), channel_id=1, source_target_pairs={{0,14},{2,0},{4,2},{6,4},{8,6},{10,8},{12,10},{14,12},{1,15},{3,1}... | collective-permute-start | bytes 983048 | tf_op jit(solution)/shard_map/ppermute | solution.py:443
  92.2 8.6 %collective-permute-done.13.refs_6_ = bf16[128,2560]{1,0:T(8,128)(2,1)S(1)} collective-permute-done((bf16[128,2560]{1,0:T(8,128)(2,1)S(1)}, bf16[128,2560]{1,0:T(8,128)(2,1)S(1)}, u32[]{:S(2)}, u32[]{:S(2)}) %collective-permute-start.13) | collective-permute-done | bytes 655392 | tf_op jit(solution)/shard_map/ppermute | solution.py:443
  100.8 4.8 %collective-permute-done.14.refs_7_ = bf16[128,2560]{1,0:T(8,128)(2,1)S(1)} collective-permute-done((bf16[128,2560]{1,0:T(8,128)(2,1)S(1)}, bf16[128,2560]{1,0:T(8,128)(2,1)S(1)}, u32[]{:S(2)}, u32[]{:S(2)}) %collective-permute-start.14) | collective-permute-done | bytes 655392 | tf_op jit(solution)/shard_map/ppermute | solution.py:443
  109.4 3.3 %collective-permute-done.18.refs_6_ = bf16[128,1280]{1,0:T(8,128)(2,1)S(1)} collective-permute-done((bf16[128,1280]{1,0:T(8,128)(2,1)S(1)}, bf16[128,1280]{1,0:T(8,128)(2,1)S(1)}, u32[]{:S(2)}, u32[]{:S(2)}) %collective-permute-start.18) | collective-permute-done | bytes 327712 | tf_op jit(solution)/shard_map/ppermute | solution.py:443
  112.7 2.2 %collective-permute-done.17.refs_5_ = bf16[128,1280]{1,0:T(8,128)(2,1)S(1)} collective-permute-done((bf16[128,1280]{1,0:T(8,128)(2,1)S(1)}, bf16[128,1280]{1,0:T(8,128)(2,1)S(1)}, u32[]{:S(2)}, u32[]{:S(2)}) %collective-permute-start.17) | collective-permute-done | bytes 327712 | tf_op jit(solution)/shard_map/ppermute | solution.py:443
  114.9 3.7 %shard_map.100 = (bf16[128,640]{1,0:T(8,128)(2,1)}, bf16[128,640]{1,0:T(8,128)(2,1)}, bf16[16,20,128]{2,1,0:T(8,128)(2,1)}) custom-call(s32[2]{0:T(128)S(1)} %pad_add_fusion.refs_0_, f32[8,128]{1,0:T(8,128)S(1)} %get-tuple-element.85.refs_1_, bf16[256,1280]{1,0:T(8,128)(2,1)S(1)} %get-tuple-element.56.refs_2_, bf16[128,1280]{1,0:T(8,128)(2,1)S(1)} %copy-done.2, ...), custom_call_target="tpu_custom_call" | custom-call | flops 838860800 | bytes 8000000 | tf_op jit(solution)/shard_map/pallas_call | solution.py:338
  118.5 12.9 %all-to-all-start = ((bf16[16,20,128]{2,1,0:T(8,128)(2,1)}), bf16[16,20,128]{2,1,0:T(8,128)(2,1)S(1)}, u32[]{:S(2)}, u32[]{:S(2)}) async-start(bf16[16,20,128]{2,1,0:T(8,128)(2,1)} %get-tuple-element.101), calls=%async_computation | async-start | bytes 196608 | tf_op jit(solution)/shard_map/all_to_all | solution.py:357
  131.9 7.9 %all-to-all-done = bf16[16,20,128]{2,1,0:T(8,128)(2,1)S(1)} async-done(((bf16[16,20,128]{2,1,0:T(8,128)(2,1)}), bf16[16,20,128]{2,1,0:T(8,128)(2,1)S(1)}, u32[]{:S(2)}, u32[]{:S(2)}) %all-to-all-start) | async-done | bytes 81952 | tf_op jit(solution)/shard_map/all_to_all | solution.py:357
  140.5 6.8 %all-to-all-start.1 = ((bf16[16,20,128]{2,1,0:T(8,128)(2,1)}), bf16[16,20,128]{2,1,0:T(8,128)(2,1)S(1)}, u32[]{:S(2)}, u32[]{:S(2)}) async-start(bf16[16,20,128]{2,1,0:T(8,128)(2,1)} %broadcast_in_dim.7), calls=%async_computation.1 | async-start | bytes 196608 | tf_op jit(solution)/shard_map/all_to_all | solution.py:353
  147.3 6.6 %all-to-all-done.1 = bf16[16,20,128]{2,1,0:T(8,128)(2,1)S(1)} async-done(((bf16[16,20,128]{2,1,0:T(8,128)(2,1)}), bf16[16,20,128]{2,1,0:T(8,128)(2,1)S(1)}, u32[]{:S(2)}, u32[]{:S(2)}) %all-to-all-start.1) | async-done | bytes 81952 | tf_op jit(solution)/shard_map/all_to_all | solution.py:353
  154.6 4.7 %all-to-all-start.2 = ((bf16[16,20,128]{2,1,0:T(8,128)(2,1)}), bf16[16,20,128]{2,1,0:T(8,128)(2,1)S(1)}, u32[]{:S(2)}, u32[]{:S(2)}) async-start(bf16[16,20,128]{2,1,0:T(8,128)(2,1)} %broadcast_in_dim.8), calls=%async_computation.2 | async-start | bytes 196608 | tf_op jit(solution)/shard_map/all_to_all | solution.py:353
  161.3 6.5 %all-to-all-done.2.blocks = bf16[16,20,128]{2,1,0:T(8,128)(2,1)S(1)} async-done(((bf16[16,20,128]{2,1,0:T(8,128)(2,1)}), bf16[16,20,128]{2,1,0:T(8,128)(2,1)S(1)}, u32[]{:S(2)}, u32[]{:S(2)}) %all-to-all-start.2) | async-done | bytes 81952 | tf_op jit(solution)/shard_map/all_to_all | solution.py:353
  (64 shorter events, 25.3 us)
Async XLA Ops:
  0.6 30.1 %collective-permute-start.6 = (bf16[128,5120]{1,0:T(8,128)(2,1)}, bf16[128,5120]{1,0:T(8,128)(2,1)}, u32[]{:S(2)}, u32[]{:S(2)}) collective-permute-start(bf16[128,5120]{1,0:T(8,128)(2,1)} %bitcast.7), channel_id=1, source_target_pairs={{0,1},{1,0},{2,3},{3,2},{4,5},{5,4},{6,7},{7,6},{8,9},{9,8},{10,11... | collective-permute-start | bytes 3932168 | tf_op jit(solution)/shard_map/ppermute | solution.py:396
  6.1 6.8 %collective-permute-start.7 = (bf16[128,2560]{1,0:T(8,128)(2,1)}, bf16[128,2560]{1,0:T(8,128)(2,1)S(1)}, u32[]{:S(2)}, u32[]{:S(2)}) collective-permute-start(bf16[128,2560]{1,0:T(8,128)(2,1)} %get-tuple-element.55), channel_id=1, source_target_pairs={{0,1},{1,0},{2,3},{3,2},{4,5},{5,4},{6,7},{7,6},{8,9},{9,8},{10,11... | collective-permute-start | bytes 1966088 | tf_op jit(solution)/shard_map/ppermute | solution.py:394
  8.4 19.0 %collective-permute-start = (bf16[128,2560]{1,0:T(8,128)(2,1)}, bf16[128,2560]{1,0:T(8,128)(2,1)}, u32[]{:S(2)}, u32[]{:S(2)}) collective-permute-start(bf16[128,2560]{1,0:T(8,128)(2,1)} %get-tuple-element.52.refs_5_), channel_id=1, source_target_pairs={{0,2},{2,4},{4,6},{6,8},{8,10},{10,12},{12,14},{14,0},{1,3},{3,5},... | collective-permute-start | bytes 1966088 | tf_op jit(solution)/shard_map/ppermute | solution.py:388
  8.5 21.8 %collective-permute-start.2 = (bf16[128,2560]{1,0:T(8,128)(2,1)}, bf16[128,2560]{1,0:T(8,128)(2,1)}, u32[]{:S(2)}, u32[]{:S(2)}) collective-permute-start(bf16[128,2560]{1,0:T(8,128)(2,1)} %get-tuple-element.53), channel_id=1, source_target_pairs={{0,15},{1,14},{2,1},{3,0},{4,3},{5,2},{6,5},{7,4},{8,7},{9,6},{10,... | collective-permute-start | bytes 1966088 | tf_op jit(solution)/shard_map/ppermute | solution.py:389
  12.8 26.5 %collective-permute-start.8 = (bf16[128,2560]{1,0:T(8,128)(2,1)}, bf16[128,2560]{1,0:T(8,128)(2,1)}, u32[]{:S(2)}, u32[]{:S(2)}) collective-permute-start(bf16[128,2560]{1,0:T(8,128)(2,1)} %get-tuple-element.53), channel_id=1, source_target_pairs={{0,1},{1,0},{2,3},{3,2},{4,5},{5,4},{6,7},{7,6},{8,9},{9,8},{10,11... | collective-permute-start | bytes 1966088 | tf_op jit(solution)/shard_map/ppermute | solution.py:390
  12.9 31.4 %collective-permute-start.4 = (bf16[128,2560]{1,0:T(8,128)(2,1)}, bf16[128,2560]{1,0:T(8,128)(2,1)}, u32[]{:S(2)}, u32[]{:S(2)}) collective-permute-start(bf16[128,2560]{1,0:T(8,128)(2,1)} %get-tuple-element.53), channel_id=1, source_target_pairs={{0,3},{1,2},{2,5},{3,4},{4,7},{5,6},{6,9},{7,8},{8,11},{9,10},{10,... | collective-permute-start | bytes 1966088 | tf_op jit(solution)/shard_map/ppermute | solution.py:391
  27.4 16.8 %collective-permute-start.5 = (bf16[128,2560]{1,0:T(8,128)(2,1)}, bf16[128,2560]{1,0:T(8,128)(2,1)}, u32[]{:S(2)}, u32[]{:S(2)}) collective-permute-start(bf16[128,2560]{1,0:T(8,128)(2,1)} %get-tuple-element.52.refs_5_), channel_id=1, source_target_pairs={{0,14},{2,0},{4,2},{6,4},{8,6},{10,8},{12,10},{14,12},{1,15},{3,1}... | collective-permute-start | bytes 1966088 | tf_op jit(solution)/shard_map/ppermute | solution.py:392
  30.4 25.0 %collective-permute-start.1 = (bf16[128,2560]{1,0:T(8,128)(2,1)}, bf16[128,2560]{1,0:T(8,128)(2,1)S(1)}, u32[]{:S(2)}, u32[]{:S(2)}) collective-permute-start(bf16[128,2560]{1,0:T(8,128)(2,1)} %collective-permute-done.refs_5_), channel_id=1, source_target_pairs={{0,2},{2,4},{4,6},{6,8},{8,10},{10,12},{12,14},{14,0},{1,3},{3,5},... | collective-permute-start | bytes 1966088 | tf_op jit(solution)/shard_map/ppermute | solution.py:404
  30.7 25.6 %collective-permute-start.3 = (bf16[128,2560]{1,0:T(8,128)(2,1)}, bf16[128,2560]{1,0:T(8,128)(2,1)S(1)}, u32[]{:S(2)}, u32[]{:S(2)}) collective-permute-start(bf16[128,2560]{1,0:T(8,128)(2,1)} %collective-permute-done.2.refs_8_), channel_id=1, source_target_pairs={{0,14},{2,0},{4,2},{6,4},{8,6},{10,8},{12,10},{14,12},{1,15},{3,1}... | collective-permute-start | bytes 1966088 | tf_op jit(solution)/shard_map/ppermute | solution.py:405
  44.3 25.2 %collective-permute-start.11 = (bf16[128,2560]{1,0:T(8,128)(2,1)}, bf16[128,2560]{1,0:T(8,128)(2,1)S(1)}, u32[]{:S(2)}, u32[]{:S(2)}) collective-permute-start(bf16[128,2560]{1,0:T(8,128)(2,1)} %collective-permute-done.4.refs_6_), channel_id=1, source_target_pairs={{0,2},{2,4},{4,6},{6,8},{8,10},{10,12},{12,14},{14,0},{1,3},{3,5},... | collective-permute-start | bytes 1966088 | tf_op jit(solution)/shard_map/ppermute | solution.py:409
  44.3 26.1 %collective-permute-start.12 = (bf16[128,2560]{1,0:T(8,128)(2,1)}, bf16[128,2560]{1,0:T(8,128)(2,1)S(1)}, u32[]{:S(2)}, u32[]{:S(2)}) collective-permute-start(bf16[128,2560]{1,0:T(8,128)(2,1)} %collective-permute-done.5.refs_7_), channel_id=1, source_target_pairs={{0,14},{2,0},{4,2},{6,4},{8,6},{10,8},{12,10},{14,12},{1,15},{3,1}... | collective-permute-start | bytes 1966088 | tf_op jit(solution)/shard_map/ppermute | solution.py:410
  56.4 28.1 %collective-permute-start.10 = (bf16[128,2560]{1,0:T(8,128)(2,1)S(1)}, bf16[128,2560]{1,0:T(8,128)(2,1)S(1)}, u32[]{:S(2)}, u32[]{:S(2)}) collective-permute-start(bf16[128,2560]{1,0:T(8,128)(2,1)S(1)} %collective-permute-done.3.refs_8_), channel_id=1, source_target_pairs={{0,14},{2,0},{4,2},{6,4},{8,6},{10,8},{12,10},{14,12},{1,15},{3,1}... | collective-permute-start | bytes 1966088 | tf_op jit(solution)/shard_map/ppermute | solution.py:419
  58.2 26.3 %collective-permute-start.9 = (bf16[128,2560]{1,0:T(8,128)(2,1)S(1)}, bf16[128,2560]{1,0:T(8,128)(2,1)S(1)}, u32[]{:S(2)}, u32[]{:S(2)}) collective-permute-start(bf16[128,2560]{1,0:T(8,128)(2,1)S(1)} %collective-permute-done.1.refs_5_), channel_id=1, source_target_pairs={{0,2},{2,4},{4,6},{6,8},{8,10},{10,12},{12,14},{14,0},{1,3},{3,5},... | collective-permute-start | bytes 1966088 | tf_op jit(solution)/shard_map/ppermute | solution.py:418
  84.7 22.0 %collective-permute-start.16 = (bf16[128,1280]{1,0:T(8,128)(2,1)S(1)}, bf16[128,1280]{1,0:T(8,128)(2,1)S(1)}, u32[]{:S(2)}, u32[]{:S(2)}) collective-permute-start(bf16[128,1280]{1,0:T(8,128)(2,1)S(1)} %pad_maximum_fusion.1), channel_id=1, source_target_pairs={{0,14},{2,0},{4,2},{6,4},{8,6},{10,8},{12,10},{14,12},{1,15},{3,1}... | collective-permute-start | bytes 983048 | tf_op jit(solution)/shard_map/ppermute | solution.py:443
  86.6 14.2 %collective-permute-start.13 = (bf16[128,2560]{1,0:T(8,128)(2,1)S(1)}, bf16[128,2560]{1,0:T(8,128)(2,1)S(1)}, u32[]{:S(2)}, u32[]{:S(2)}) collective-permute-start(bf16[128,2560]{1,0:T(8,128)(2,1)S(1)} %collective-permute-done.11.refs_6_), channel_id=1, source_target_pairs={{0,2},{2,4},{4,6},{6,8},{8,10},{10,12},{12,14},{14,0},{1,3},{3,5},... | collective-permute-start | bytes 1966088 | tf_op jit(solution)/shard_map/ppermute | solution.py:443
  86.6 19.1 %collective-permute-start.14 = (bf16[128,2560]{1,0:T(8,128)(2,1)S(1)}, bf16[128,2560]{1,0:T(8,128)(2,1)S(1)}, u32[]{:S(2)}, u32[]{:S(2)}) collective-permute-start(bf16[128,2560]{1,0:T(8,128)(2,1)S(1)} %collective-permute-done.12.refs_7_), channel_id=1, source_target_pairs={{0,14},{2,0},{4,2},{6,4},{8,6},{10,8},{12,10},{14,12},{1,15},{3,1}... | collective-permute-start | bytes 1966088 | tf_op jit(solution)/shard_map/ppermute | solution.py:443
  89.3 18.6 %collective-permute-start.15 = (bf16[128,1280]{1,0:T(8,128)(2,1)S(1)}, bf16[128,1280]{1,0:T(8,128)(2,1)S(1)}, u32[]{:S(2)}, u32[]{:S(2)}) collective-permute-start(bf16[128,1280]{1,0:T(8,128)(2,1)S(1)} %pad_maximum_fusion), channel_id=1, source_target_pairs={{0,2},{2,4},{4,6},{6,8},{8,10},{10,12},{12,14},{14,0},{1,3},{3,5},... | collective-permute-start | bytes 983048 | tf_op jit(solution)/shard_map/ppermute | solution.py:443
  89.4 23.3 %collective-permute-start.18 = (bf16[128,1280]{1,0:T(8,128)(2,1)S(1)}, bf16[128,1280]{1,0:T(8,128)(2,1)S(1)}, u32[]{:S(2)}, u32[]{:S(2)}) collective-permute-start(bf16[128,1280]{1,0:T(8,128)(2,1)S(1)} %pad_maximum_fusion.3), channel_id=1, source_target_pairs={{0,14},{2,0},{4,2},{6,4},{8,6},{10,8},{12,10},{14,12},{1,15},{3,1}... | collective-permute-start | bytes 983048 | tf_op jit(solution)/shard_map/ppermute | solution.py:443
  100.8 14.0 %collective-permute-start.17 = (bf16[128,1280]{1,0:T(8,128)(2,1)S(1)}, bf16[128,1280]{1,0:T(8,128)(2,1)S(1)}, u32[]{:S(2)}, u32[]{:S(2)}) collective-permute-start(bf16[128,1280]{1,0:T(8,128)(2,1)S(1)} %pad_maximum_fusion.2), channel_id=1, source_target_pairs={{0,2},{2,4},{4,6},{6,8},{8,10},{10,12},{12,14},{14,0},{1,3},{3,5},... | collective-permute-start | bytes 983048 | tf_op jit(solution)/shard_map/ppermute | solution.py:443
  118.5 21.3 %all-to-all-start = ((bf16[16,20,128]{2,1,0:T(8,128)(2,1)}), bf16[16,20,128]{2,1,0:T(8,128)(2,1)S(1)}, u32[]{:S(2)}, u32[]{:S(2)}) async-start(bf16[16,20,128]{2,1,0:T(8,128)(2,1)} %get-tuple-element.101), calls=%async_computation | async-start | bytes 196608 | tf_op jit(solution)/shard_map/all_to_all | solution.py:357
  131.4 27.9 %collective-permute-start.20 = (bf16[128,640]{1,0:T(8,128)(2,1)}, bf16[128,640]{1,0:T(8,128)(2,1)S(1)}, u32[]{:S(2)}, u32[]{:S(2)}) collective-permute-start(bf16[128,640]{1,0:T(8,128)(2,1)} %get-tuple-element.100), channel_id=1, source_target_pairs={{0,1},{1,0},{2,3},{3,2},{4,5},{5,4},{6,7},{7,6},{8,9},{9,8},{10,11... | collective-permute-start | bytes 491528 | tf_op jit(solution)/shard_map/ppermute | solution.py:433
  131.6 27.7 %collective-permute-start.19 = (bf16[128,640]{1,0:T(8,128)(2,1)}, bf16[128,640]{1,0:T(8,128)(2,1)S(1)}, u32[]{:S(2)}, u32[]{:S(2)}) collective-permute-start(bf16[128,640]{1,0:T(8,128)(2,1)} %get-tuple-element.99), channel_id=1, source_target_pairs={{0,1},{1,0},{2,3},{3,2},{4,5},{5,4},{6,7},{7,6},{8,9},{9,8},{10,11... | collective-permute-start | bytes 491528 | tf_op jit(solution)/shard_map/ppermute | solution.py:433
  140.5 13.4 %all-to-all-start.1 = ((bf16[16,20,128]{2,1,0:T(8,128)(2,1)}), bf16[16,20,128]{2,1,0:T(8,128)(2,1)S(1)}, u32[]{:S(2)}, u32[]{:S(2)}) async-start(bf16[16,20,128]{2,1,0:T(8,128)(2,1)} %broadcast_in_dim.7), calls=%async_computation.1 | async-start | bytes 196608 | tf_op jit(solution)/shard_map/all_to_all | solution.py:353
  154.6 13.2 %all-to-all-start.2 = ((bf16[16,20,128]{2,1,0:T(8,128)(2,1)}), bf16[16,20,128]{2,1,0:T(8,128)(2,1)S(1)}, u32[]{:S(2)}, u32[]{:S(2)}) async-start(bf16[16,20,128]{2,1,0:T(8,128)(2,1)} %broadcast_in_dim.8), calls=%async_computation.2 | async-start | bytes 196608 | tf_op jit(solution)/shard_map/all_to_all | solution.py:353
  (8 other events, 139.2 us)
where the time goes:
time: 169 us; the launch traced here: 168 us
  waiting for transfers between devices  87.8 us (52%)
  starting transfers between devices  48.6 us (29%)
  Pallas kernels  23.9 us (14%)
  local copies, waits for them, and re-layouts  4.97 us (3%)
  other arithmetic  2.22 us (1%)
    ppermute x6, waiting for transfers between devices, moved(): return lax.ppermute(value, 'z', pairs)  20.1 us
    pallas_call x6, Pallas kernels, attend(): pl.pallas_call(functools.partial(attend_body, kind=kind, reach=reach, hea...  14.6 us
    ppermute x1, waiting for transfers between devices, shards(): fa = [a0, lax.ppermute(a0, 'z', ahead)]  14.5 us
    all_to_all x2, waiting for transfers between devices, sent(): return lax.all_to_all(copies, axis, 0, 0, tiled=True)  13.1 us
    ppermute x1, waiting for transfers between devices, shards(): kb.append(lax.ppermute(y, 'z', back))  13 us
    all_to_all x1, starting transfers between devices, total_of(): lax.all_to_all(blocks, SEQ, 0, 0, tiled=True).astype(f32).sum(axis=0)  12.9 us
    all_to_all x2, starting transfers between devices, sent(): return lax.all_to_all(copies, axis, 0, 0, tiled=True)  11.4 us
    ppermute x1, waiting for transfers between devices, shards(): fb.append(lax.ppermute(x, 'z', ahead))  11.2 us
  transfers between devices with their start and end apart: 24, of which 14 were waited for; matrix products, arithmetic and copies ran while one was open for 3% of the time, Pallas kernels for 12%

commit v1 on v0

--- a/solution.py
+++ b/solution.py
@@ -81,8 +81,11 @@
     return (col // RANK == e).astype(f32)
 
 
-def query_body(tok_mine, tok_other, down, gate, up, mine, other, query, low_out, gates_out):
+def query_body(
+    tok_mine, tok_other, down, gate, up, mine, other, query, low_out, gates_out, tok_kept
+):
     rows = tok_mine.shape[0]
+    tok_kept[...] = tok_other[...]
     half = up.shape[1]
     spread = expert_columns(down.shape[1])
     for part, tok, base in ((0, tok_mine, mine), (1, tok_other, other)):
@@ -106,11 +109,12 @@
     return pl.pallas_call(
         query_body,
         in_specs=[WHOLE] * 7,
-        out_specs=[WHOLE] * 3,
+        out_specs=[WHOLE] * 4,
         out_shape=[
             jax.ShapeDtypeStruct((rows, half), bf16),
             jax.ShapeDtypeStruct((rows, down.shape[1]), bf16),
             jax.ShapeDtypeStruct((EXPERTS, rows), f32),
+            pltpu.VMEM(tok_other.shape, tok_other.dtype),
         ],
         name="query",
         compiler_params=pltpu.CompilerParams(vmem_limit_bytes=VMEM_LIMIT),
@@ -385,18 +389,18 @@
         return [(2 * i + c, 2 * ((i + way) % n) + 1 - c) for i in range(n) for c in range(2)]
 
     a0, other_kv = pack(k_base, v_base)
-    fa = [a0, lax.ppermute(a0, "z", ahead)]
-    kb = [None, lax.ppermute(other_kv, SEQ, cross(-1))]
+    fa = [a0, moved(a0, ahead)]
+    kb = [None, moved(other_kv, cross(-1), SEQ)]
     b0 = lax.ppermute(other_kv, "c", swap)
     fb = [b0, lax.ppermute(other_kv, SEQ, cross(1))]
     ka = [a0, lax.ppermute(a0, "z", back)]
     mine_qc, other_qc = pack(base_query, cotangent)
     qc = lax.ppermute(other_qc, "c", swap)
     tok_mine = tokens[0]
-    tok_other = lax.ppermute(tok_mine, "c", swap)
+    tok_other = moved(tok_mine, swap, "c")
 
     up_half = lax.dynamic_slice_in_dim(up_weight, core * half, half, 1)
-    query, low, gates = make_query(
+    query, low, gates, tok_other = make_query(
         tok_mine, tok_other, adapter_down, gate_weight, up_half, mine_qc, qc
     )
     cot_mine = mine_qc[:, half:]
@@ -421,8 +425,10 @@
             fb.append(moved(fb[d + 1], ahead))
             ka.append(moved(ka[d + 1], back))
     parts = []
-    for j in range(2):
-        cut = [head_part(p, j) for p in (x, y)]
+    heads = half // HEAD_DIM
+    split = heads // 2 + heads % 4 // 2
+    for start, stop in ((0, split), (split, heads)):
+        cut = [head_part(p, start, stop) for p in (x, y)]
         parts.append((moved(cut[0], ahead), moved(cut[1], back)))
     common = tuple(in_vmem(v) for v in common)
     state = [in_vmem(v) for v in state]
@@ -439,15 +445,14 @@
     return attended[None], total_of(grad, (EXPERTS, tokens.shape[2]))
 
 
-def moved(value, pairs):
-    return lax.ppermute(value, "z", pairs)
-
-
-def head_part(piece, j):
-    width = piece.shape[1] // 4
-    keys = piece[:, j * width : (j + 1) * width]
-    values = piece[:, (2 + j) * width : (3 + j) * width]
-    return jnp.concatenate([keys, values], axis=1)
+def moved(value, pairs, axis="z"):
+    return lax.ppermute(value, axis, pairs)
+
+
+def head_part(piece, start, stop):
+    half = piece.shape[1] // 2
+    a, b = start * HEAD_DIM, stop * HEAD_DIM
+    return jnp.concatenate([piece[:, a:b], piece[:, half + a : half + b]], axis=1)
 
 
 def solution(mesh):

time: 169 us -> 169 us (level)
  no operation moved by 1% of the time
where the time goes in v1:
time: 169 us; the launch traced here: 168 us
  waiting for transfers between devices  87.4 us (52%)
  starting transfers between devices  49.6 us (29%)
  Pallas kernels  23.2 us (14%)
  local copies, waits for them, and re-layouts  4.93 us (3%)
  other arithmetic  2.36 us (1%)
    ppermute x9, waiting for transfers between devices, moved(): return lax.ppermute(value, axis, pairs)  34.4 us
    ppermute x9, starting transfers between devices, moved(): return lax.ppermute(value, axis, pairs)  15 us
    all_to_all x1, starting transfers between devices, total_of(): lax.all_to_all(blocks, SEQ, 0, 0, tiled=True).astype(f32).sum(axis=0)  13.8 us
    pallas_call x6, Pallas kernels, attend(): pl.pallas_call(functools.partial(attend_body, kind=kind, reach=reach, hea...  13.8 us
    ppermute x1, waiting for transfers between devices, shards(): kb.append(lax.ppermute(y, 'z', back))  13 us
    all_to_all x2, waiting for transfers between devices, sent(): return lax.all_to_all(copies, axis, 0, 0, tiled=True)  12.9 us
    all_to_all x2, starting transfers between devices, sent(): return lax.all_to_all(copies, axis, 0, 0, tiled=True)  11.4 us
    ppermute x1, waiting for transfers between devices, shards(): fb.append(lax.ppermute(x, 'z', ahead))  11.2 us
  transfers between devices with their start and end apart: 24, of which 14 were waited for; matrix products, arithmetic and copies ran while one was open for 3% of the time, Pallas kernels for 12%

profile of v1, /device:TPU:1, one launch (start us, length us, event | category | flops | bytes accessed | tf_op | source)
XLA Modules:
  0.0 168.4 jit_solution(177781287633806375)
XLA Ops:
  0.6 3.3 %collective-permute-start.6 = (bf16[128,5120]{1,0:T(8,128)(2,1)}, bf16[128,5120]{1,0:T(8,128)(2,1)}, u32[]{:S(2)}, u32[]{:S(2)}) collective-permute-start(bf16[128,5120]{1,0:T(8,128)(2,1)} %bitcast.7), channel_id=1, source_target_pairs={{0,1},{1,0},{2,3},{3,2},{4,5},{5,4},{6,7},{7,6},{8,9},{9,8},{10,11... | collective-permute-start | bytes 3932168 | tf_op jit(solution)/shard_map/ppermute | solution.py:449
  6.3 2.2 %pack.2 = (bf16[128,2560]{1,0:T(8,128)(2,1)}, bf16[128,2560]{1,0:T(8,128)(2,1)}) custom-call(bf16[1,128,2560]{2,1,0:T(8,128)(2,1)} %a.2, bf16[1,128,2560]{2,1,0:T(8,128)(2,1)} %b.2), custom_call_target="tpu_custom_call" | custom-call | flops 2000000 | bytes 5000000 | tf_op jit(solution)/shard_map/pack/pallas_call | solution.py:63
  8.5 4.2 %collective-permute-start.2 = (bf16[128,2560]{1,0:T(8,128)(2,1)}, bf16[128,2560]{1,0:T(8,128)(2,1)}, u32[]{:S(2)}, u32[]{:S(2)}) collective-permute-start(bf16[128,2560]{1,0:T(8,128)(2,1)} %get-tuple-element.54), channel_id=1, source_target_pairs={{0,15},{1,14},{2,1},{3,0},{4,3},{5,2},{6,5},{7,4},{8,7},{9,6},{10,... | collective-permute-start | bytes 1966088 | tf_op jit(solution)/shard_map/ppermute | solution.py:449
  12.9 14.5 %collective-permute-done.refs_5_ = bf16[128,2560]{1,0:T(8,128)(2,1)} collective-permute-done((bf16[128,2560]{1,0:T(8,128)(2,1)}, bf16[128,2560]{1,0:T(8,128)(2,1)}, u32[]{:S(2)}, u32[]{:S(2)}) %collective-permute-start) | collective-permute-done | bytes 655392 | tf_op jit(solution)/shard_map/ppermute | solution.py:449
  30.7 2.4 %collective-permute-start.3 = (bf16[128,2560]{1,0:T(8,128)(2,1)}, bf16[128,2560]{1,0:T(8,128)(2,1)S(1)}, u32[]{:S(2)}, u32[]{:S(2)}) collective-permute-start(bf16[128,2560]{1,0:T(8,128)(2,1)} %collective-permute-done.2.refs_8_), channel_id=1, source_target_pairs={{0,14},{2,0},{4,2},{6,4},{8,6},{10,8},{12,10},{14,12},{1,15},{3,1}... | collective-permute-start | bytes 1966088 | tf_op jit(solution)/shard_map/ppermute | solution.py:409
  35.0 4.4 %query.1 = (bf16[256,1280]{1,0:T(8,128)(2,1)S(1)}, bf16[256,256]{1,0:T(8,128)(2,1)S(1)}, f32[8,256]{1,0:T(8,128)S(1)}, bf16[128,5120]{1,0:T(8,128)(2,1)S(1)}) custom-call(bf16[128,5120]{1,0:T(8,128)(2,1)S(1)} %bitcast.8, bf16[128,5120]{1,0:T(8,128)(2,1)} %collective-permute-done.6.tok_other, bf16[5120,256]{1,0:T(8,128)(2,1)S(1)} %copy-done.3, ...), custom_call_target="tpu_custom_call" | custom-call | flops 838860800 | bytes 8000000 | tf_op jit(solution)/shard_map/query/pallas_call | solution.py:109
  39.4 4.9 %shard_map.95 = (f32[8,128]{1,0:T(8,128)S(1)}, f32[256,1280]{1,0:T(8,128)S(1)}, f32[256,1280]{1,0:T(8,128)S(1)}, f32[256,1280]{1,0:T(8,128)S(1)}, f32[256,1280]{...) custom-call(s32[2]{0:T(128)S(1)} %pad_add_fusion.refs_0_, f32[8,128]{1,0:T(8,128)S(1)} %broadcast_in_dim.6.refs_1_, ...), custom_call_target="tpu_custom_call" | custom-call | flops 1677721600 | bytes 8000000 | tf_op jit(solution)/shard_map/pallas_call | solution.py:342
  44.4 2.7 %collective-permute-start.12 = (bf16[128,2560]{1,0:T(8,128)(2,1)}, bf16[128,2560]{1,0:T(8,128)(2,1)S(1)}, u32[]{:S(2)}, u32[]{:S(2)}) collective-permute-start(bf16[128,2560]{1,0:T(8,128)(2,1)} %collective-permute-done.5.refs_7_), channel_id=1, source_target_pairs={{0,14},{2,0},{4,2},{6,4},{8,6},{10,8},{12,10},{14,12},{1,15},{3,1}... | collective-permute-start | bytes 1966088 | tf_op jit(solution)/shard_map/ppermute | solution.py:414
  47.1 2.4 %shard_map.96 = (f32[8,128]{1,0:T(8,128)S(1)}, f32[256,1280]{1,0:T(8,128)S(1)}, f32[256,1280]{1,0:T(8,128)S(1)}, f32[256,1280]{1,0:T(8,128)S(1)}, f32[256,1280]{...) custom-call(s32[2]{0:T(128)S(1)} %pad_add_fusion.refs_0_, f32[8,128]{1,0:T(8,128)S(1)} %get-tuple-element.59.refs_1_, ...), custom_call_target="tpu_custom_call" | custom-call | flops 3355443200 | bytes 8000000 | tf_op jit(solution)/shard_map/pallas_call | solution.py:342
  49.5 5.9 %collective-permute-done.1.refs_5_ = bf16[128,2560]{1,0:T(8,128)(2,1)S(1)} collective-permute-done((bf16[128,2560]{1,0:T(8,128)(2,1)}, bf16[128,2560]{1,0:T(8,128)(2,1)S(1)}, u32[]{:S(2)}, u32[]{:S(2)}) %collective-permute-start.1) | collective-permute-done | bytes 655392 | tf_op jit(solution)/shard_map/ppermute | solution.py:408
  58.2 11.2 %collective-permute-done.11.refs_6_ = bf16[128,2560]{1,0:T(8,128)(2,1)S(1)} collective-permute-done((bf16[128,2560]{1,0:T(8,128)(2,1)}, bf16[128,2560]{1,0:T(8,128)(2,1)S(1)}, u32[]{:S(2)}, u32[]{:S(2)}) %collective-permute-start.11) | collective-permute-done | bytes 655392 | tf_op jit(solution)/shard_map/ppermute | solution.py:413
  71.5 13.0 %collective-permute-done.10.refs_8_ = bf16[128,2560]{1,0:T(8,128)(2,1)S(1)} collective-permute-done((bf16[128,2560]{1,0:T(8,128)(2,1)S(1)}, bf16[128,2560]{1,0:T(8,128)(2,1)S(1)}, u32[]{:S(2)}, u32[]{:S(2)}) %collective-permute-start.10) | collective-permute-done | bytes 655392 | tf_op jit(solution)/shard_map/ppermute | solution.py:423
  86.5 2.7 %collective-permute-start.14 = (bf16[128,2560]{1,0:T(8,128)(2,1)S(1)}, bf16[128,2560]{1,0:T(8,128)(2,1)S(1)}, u32[]{:S(2)}, u32[]{:S(2)}) collective-permute-start(bf16[128,2560]{1,0:T(8,128)(2,1)S(1)} %collective-permute-done.12.refs_7_), channel_id=1, source_target_pairs={{0,14},{2,0},{4,2},{6,4},{8,6},{10,8},{12,10},{14,12},{1,15},{3,1}... | collective-permute-start | bytes 1966088 | tf_op jit(solution)/shard_map/ppermute | solution.py:449
  89.4 2.7 %collective-permute-start.18 = (bf16[128,1024]{1,0:T(8,128)(2,1)S(1)}, bf16[128,1024]{1,0:T(8,128)(2,1)S(1)}, u32[]{:S(2)}, u32[]{:S(2)}) collective-permute-start(bf16[128,1024]{1,0:T(8,128)(2,1)S(1)} %pad_maximum_fusion.3), channel_id=1, source_target_pairs={{0,14},{2,0},{4,2},{6,4},{8,6},{10,8},{12,10},{14,12},{1,15},{3,1}... | collective-permute-start | bytes 786440 | tf_op jit(solution)/shard_map/ppermute | solution.py:449
  92.1 8.6 %collective-permute-done.13.refs_6_ = bf16[128,2560]{1,0:T(8,128)(2,1)S(1)} collective-permute-done((bf16[128,2560]{1,0:T(8,128)(2,1)S(1)}, bf16[128,2560]{1,0:T(8,128)(2,1)S(1)}, u32[]{:S(2)}, u32[]{:S(2)}) %collective-permute-start.13) | collective-permute-done | bytes 655392 | tf_op jit(solution)/shard_map/ppermute | solution.py:449
  100.7 6.2 %collective-permute-done.14.refs_7_ = bf16[128,2560]{1,0:T(8,128)(2,1)S(1)} collective-permute-done((bf16[128,2560]{1,0:T(8,128)(2,1)S(1)}, bf16[128,2560]{1,0:T(8,128)(2,1)S(1)}, u32[]{:S(2)}, u32[]{:S(2)}) %collective-permute-start.14) | collective-permute-done | bytes 655392 | tf_op jit(solution)/shard_map/ppermute | solution.py:449
  112.6 2.2 %collective-permute-done.17.refs_5_ = bf16[128,1024]{1,0:T(8,128)(2,1)S(1)} collective-permute-done((bf16[128,1024]{1,0:T(8,128)(2,1)S(1)}, bf16[128,1024]{1,0:T(8,128)(2,1)S(1)}, u32[]{:S(2)}, u32[]{:S(2)}) %collective-permute-start.17) | collective-permute-done | bytes 262176 | tf_op jit(solution)/shard_map/ppermute | solution.py:449
  114.8 2.7 %shard_map.100 = (bf16[128,512]{1,0:T(8,128)(2,1)}, bf16[128,512]{1,0:T(8,128)(2,1)}, bf16[16,20,128]{2,1,0:T(8,128)(2,1)}) custom-call(s32[2]{0:T(128)S(1)} %pad_add_fusion.refs_0_, f32[8,128]{1,0:T(8,128)S(1)} %get-tuple-element.86.refs_1_, bf16[256,1280]{1,0:T(8,128)(2,1)S(1)} %get-tuple-element.57.refs_2_, bf16[128,1280]{1,0:T(8,128)(2,1)S(1)} %copy-done.2, ...), custom_call_target="tpu_custom_call" | custom-call | flops 671088640 | bytes 8000000 | tf_op jit(solution)/shard_map/pallas_call | solution.py:342
  117.5 13.8 %all-to-all-start = ((bf16[16,20,128]{2,1,0:T(8,128)(2,1)}), bf16[16,20,128]{2,1,0:T(8,128)(2,1)S(1)}, u32[]{:S(2)}, u32[]{:S(2)}) async-start(bf16[16,20,128]{2,1,0:T(8,128)(2,1)} %get-tuple-element.103), calls=%async_computation | async-start | bytes 196608 | tf_op jit(solution)/shard_map/all_to_all | solution.py:361
  131.8 7.9 %all-to-all-done = bf16[16,20,128]{2,1,0:T(8,128)(2,1)S(1)} async-done(((bf16[16,20,128]{2,1,0:T(8,128)(2,1)}), bf16[16,20,128]{2,1,0:T(8,128)(2,1)S(1)}, u32[]{:S(2)}, u32[]{:S(2)}) %all-to-all-start) | async-done | bytes 81952 | tf_op jit(solution)/shard_map/all_to_all | solution.py:361
  140.4 6.8 %all-to-all-start.1 = ((bf16[16,20,128]{2,1,0:T(8,128)(2,1)}), bf16[16,20,128]{2,1,0:T(8,128)(2,1)S(1)}, u32[]{:S(2)}, u32[]{:S(2)}) async-start(bf16[16,20,128]{2,1,0:T(8,128)(2,1)} %broadcast_in_dim.7), calls=%async_computation.1 | async-start | bytes 196608 | tf_op jit(solution)/shard_map/all_to_all | solution.py:357
  147.2 6.6 %all-to-all-done.1 = bf16[16,20,128]{2,1,0:T(8,128)(2,1)S(1)} async-done(((bf16[16,20,128]{2,1,0:T(8,128)(2,1)}), bf16[16,20,128]{2,1,0:T(8,128)(2,1)S(1)}, u32[]{:S(2)}, u32[]{:S(2)}) %all-to-all-start.1) | async-done | bytes 81952 | tf_op jit(solution)/shard_map/all_to_all | solution.py:357
  154.5 4.7 %all-to-all-start.2 = ((bf16[16,20,128]{2,1,0:T(8,128)(2,1)}), bf16[16,20,128]{2,1,0:T(8,128)(2,1)S(1)}, u32[]{:S(2)}, u32[]{:S(2)}) async-start(bf16[16,20,128]{2,1,0:T(8,128)(2,1)} %broadcast_in_dim.8), calls=%async_computation.2 | async-start | bytes 196608 | tf_op jit(solution)/shard_map/all_to_all | solution.py:357
  161.3 6.3 %all-to-all-done.2.blocks = bf16[16,20,128]{2,1,0:T(8,128)(2,1)S(1)} async-done(((bf16[16,20,128]{2,1,0:T(8,128)(2,1)}), bf16[16,20,128]{2,1,0:T(8,128)(2,1)S(1)}, u32[]{:S(2)}, u32[]{:S(2)}) %all-to-all-start.2) | async-done | bytes 81952 | tf_op jit(solution)/shard_map/all_to_all | solution.py:357
  (63 shorter events, 25.1 us)
Async XLA Ops:
  0.6 30.1 %collective-permute-start.6 = (bf16[128,5120]{1,0:T(8,128)(2,1)}, bf16[128,5120]{1,0:T(8,128)(2,1)}, u32[]{:S(2)}, u32[]{:S(2)}) collective-permute-start(bf16[128,5120]{1,0:T(8,128)(2,1)} %bitcast.7), channel_id=1, source_target_pairs={{0,1},{1,0},{2,3},{3,2},{4,5},{5,4},{6,7},{7,6},{8,9},{9,8},{10,11... | collective-permute-start | bytes 3932168 | tf_op jit(solution)/shard_map/ppermute | solution.py:449
  6.1 6.8 %collective-permute-start.7 = (bf16[128,2560]{1,0:T(8,128)(2,1)}, bf16[128,2560]{1,0:T(8,128)(2,1)S(1)}, u32[]{:S(2)}, u32[]{:S(2)}) collective-permute-start(bf16[128,2560]{1,0:T(8,128)(2,1)} %get-tuple-element.56), channel_id=1, source_target_pairs={{0,1},{1,0},{2,3},{3,2},{4,5},{5,4},{6,7},{7,6},{8,9},{9,8},{10,11... | collective-permute-start | bytes 1966088 | tf_op jit(solution)/shard_map/ppermute | solution.py:398
  8.4 19.0 %collective-permute-start = (bf16[128,2560]{1,0:T(8,128)(2,1)}, bf16[128,2560]{1,0:T(8,128)(2,1)}, u32[]{:S(2)}, u32[]{:S(2)}) collective-permute-start(bf16[128,2560]{1,0:T(8,128)(2,1)} %get-tuple-element.53.refs_5_), channel_id=1, source_target_pairs={{0,2},{2,4},{4,6},{6,8},{8,10},{10,12},{12,14},{14,0},{1,3},{3,5},... | collective-permute-start | bytes 1966088 | tf_op jit(solution)/shard_map/ppermute | solution.py:449
  8.5 21.8 %collective-permute-start.2 = (bf16[128,2560]{1,0:T(8,128)(2,1)}, bf16[128,2560]{1,0:T(8,128)(2,1)}, u32[]{:S(2)}, u32[]{:S(2)}) collective-permute-start(bf16[128,2560]{1,0:T(8,128)(2,1)} %get-tuple-element.54), channel_id=1, source_target_pairs={{0,15},{1,14},{2,1},{3,0},{4,3},{5,2},{6,5},{7,4},{8,7},{9,6},{10,... | collective-permute-start | bytes 1966088 | tf_op jit(solution)/shard_map/ppermute | solution.py:449
  12.8 26.6 %collective-permute-start.8 = (bf16[128,2560]{1,0:T(8,128)(2,1)}, bf16[128,2560]{1,0:T(8,128)(2,1)}, u32[]{:S(2)}, u32[]{:S(2)}) collective-permute-start(bf16[128,2560]{1,0:T(8,128)(2,1)} %get-tuple-element.54), channel_id=1, source_target_pairs={{0,1},{1,0},{2,3},{3,2},{4,5},{5,4},{6,7},{7,6},{8,9},{9,8},{10,11... | collective-permute-start | bytes 1966088 | tf_op jit(solution)/shard_map/ppermute | solution.py:394
  12.9 31.4 %collective-permute-start.4 = (bf16[128,2560]{1,0:T(8,128)(2,1)}, bf16[128,2560]{1,0:T(8,128)(2,1)}, u32[]{:S(2)}, u32[]{:S(2)}) collective-permute-start(bf16[128,2560]{1,0:T(8,128)(2,1)} %get-tuple-element.54), channel_id=1, source_target_pairs={{0,3},{1,2},{2,5},{3,4},{4,7},{5,6},{6,9},{7,8},{8,11},{9,10},{10,... | collective-permute-start | bytes 1966088 | tf_op jit(solution)/shard_map/ppermute | solution.py:395
  27.4 16.9 %collective-permute-start.5 = (bf16[128,2560]{1,0:T(8,128)(2,1)}, bf16[128,2560]{1,0:T(8,128)(2,1)}, u32[]{:S(2)}, u32[]{:S(2)}) collective-permute-start(bf16[128,2560]{1,0:T(8,128)(2,1)} %get-tuple-element.53.refs_5_), channel_id=1, source_target_pairs={{0,14},{2,0},{4,2},{6,4},{8,6},{10,8},{12,10},{14,12},{1,15},{3,1}... | collective-permute-start | bytes 1966088 | tf_op jit(solution)/shard_map/ppermute | solution.py:396
  30.4 25.0 %collective-permute-start.1 = (bf16[128,2560]{1,0:T(8,128)(2,1)}, bf16[128,2560]{1,0:T(8,128)(2,1)S(1)}, u32[]{:S(2)}, u32[]{:S(2)}) collective-permute-start(bf16[128,2560]{1,0:T(8,128)(2,1)} %collective-permute-done.refs_5_), channel_id=1, source_target_pairs={{0,2},{2,4},{4,6},{6,8},{8,10},{10,12},{12,14},{14,0},{1,3},{3,5},... | collective-permute-start | bytes 1966088 | tf_op jit(solution)/shard_map/ppermute | solution.py:408
  30.7 25.6 %collective-permute-start.3 = (bf16[128,2560]{1,0:T(8,128)(2,1)}, bf16[128,2560]{1,0:T(8,128)(2,1)S(1)}, u32[]{:S(2)}, u32[]{:S(2)}) collective-permute-start(bf16[128,2560]{1,0:T(8,128)(2,1)} %collective-permute-done.2.refs_8_), channel_id=1, source_target_pairs={{0,14},{2,0},{4,2},{6,4},{8,6},{10,8},{12,10},{14,12},{1,15},{3,1}... | collective-permute-start | bytes 1966088 | tf_op jit(solution)/shard_map/ppermute | solution.py:409
  44.3 25.1 %collective-permute-start.11 = (bf16[128,2560]{1,0:T(8,128)(2,1)}, bf16[128,2560]{1,0:T(8,128)(2,1)S(1)}, u32[]{:S(2)}, u32[]{:S(2)}) collective-permute-start(bf16[128,2560]{1,0:T(8,128)(2,1)} %collective-permute-done.4.refs_6_), channel_id=1, source_target_pairs={{0,2},{2,4},{4,6},{6,8},{8,10},{10,12},{12,14},{14,0},{1,3},{3,5},... | collective-permute-start | bytes 1966088 | tf_op jit(solution)/shard_map/ppermute | solution.py:413
  44.4 26.0 %collective-permute-start.12 = (bf16[128,2560]{1,0:T(8,128)(2,1)}, bf16[128,2560]{1,0:T(8,128)(2,1)S(1)}, u32[]{:S(2)}, u32[]{:S(2)}) collective-permute-start(bf16[128,2560]{1,0:T(8,128)(2,1)} %collective-permute-done.5.refs_7_), channel_id=1, source_target_pairs={{0,14},{2,0},{4,2},{6,4},{8,6},{10,8},{12,10},{14,12},{1,15},{3,1}... | collective-permute-start | bytes 1966088 | tf_op jit(solution)/shard_map/ppermute | solution.py:414
  56.4 28.1 %collective-permute-start.10 = (bf16[128,2560]{1,0:T(8,128)(2,1)S(1)}, bf16[128,2560]{1,0:T(8,128)(2,1)S(1)}, u32[]{:S(2)}, u32[]{:S(2)}) collective-permute-start(bf16[128,2560]{1,0:T(8,128)(2,1)S(1)} %collective-permute-done.3.refs_8_), channel_id=1, source_target_pairs={{0,14},{2,0},{4,2},{6,4},{8,6},{10,8},{12,10},{14,12},{1,15},{3,1}... | collective-permute-start | bytes 1966088 | tf_op jit(solution)/shard_map/ppermute | solution.py:423
  58.2 26.3 %collective-permute-start.9 = (bf16[128,2560]{1,0:T(8,128)(2,1)S(1)}, bf16[128,2560]{1,0:T(8,128)(2,1)S(1)}, u32[]{:S(2)}, u32[]{:S(2)}) collective-permute-start(bf16[128,2560]{1,0:T(8,128)(2,1)S(1)} %collective-permute-done.1.refs_5_), channel_id=1, source_target_pairs={{0,2},{2,4},{4,6},{6,8},{8,10},{10,12},{12,14},{14,0},{1,3},{3,5},... | collective-permute-start | bytes 1966088 | tf_op jit(solution)/shard_map/ppermute | solution.py:422
  84.6 23.5 %collective-permute-start.16 = (bf16[128,1536]{1,0:T(8,128)(2,1)S(1)}, bf16[128,1536]{1,0:T(8,128)(2,1)S(1)}, u32[]{:S(2)}, u32[]{:S(2)}) collective-permute-start(bf16[128,1536]{1,0:T(8,128)(2,1)S(1)} %pad_maximum_fusion.1), channel_id=1, source_target_pairs={{0,14},{2,0},{4,2},{6,4},{8,6},{10,8},{12,10},{14,12},{1,15},{3,1}... | collective-permute-start | bytes 1179656 | tf_op jit(solution)/shard_map/ppermute | solution.py:449
  86.5 14.2 %collective-permute-start.13 = (bf16[128,2560]{1,0:T(8,128)(2,1)S(1)}, bf16[128,2560]{1,0:T(8,128)(2,1)S(1)}, u32[]{:S(2)}, u32[]{:S(2)}) collective-permute-start(bf16[128,2560]{1,0:T(8,128)(2,1)S(1)} %collective-permute-done.11.refs_6_), channel_id=1, source_target_pairs={{0,2},{2,4},{4,6},{6,8},{8,10},{10,12},{12,14},{14,0},{1,3},{3,5},... | collective-permute-start | bytes 1966088 | tf_op jit(solution)/shard_map/ppermute | solution.py:449
  86.5 20.5 %collective-permute-start.14 = (bf16[128,2560]{1,0:T(8,128)(2,1)S(1)}, bf16[128,2560]{1,0:T(8,128)(2,1)S(1)}, u32[]{:S(2)}, u32[]{:S(2)}) collective-permute-start(bf16[128,2560]{1,0:T(8,128)(2,1)S(1)} %collective-permute-done.12.refs_7_), channel_id=1, source_target_pairs={{0,14},{2,0},{4,2},{6,4},{8,6},{10,8},{12,10},{14,12},{1,15},{3,1}... | collective-permute-start | bytes 1966088 | tf_op jit(solution)/shard_map/ppermute | solution.py:449
  89.2 20.0 %collective-permute-start.15 = (bf16[128,1536]{1,0:T(8,128)(2,1)S(1)}, bf16[128,1536]{1,0:T(8,128)(2,1)S(1)}, u32[]{:S(2)}, u32[]{:S(2)}) collective-permute-start(bf16[128,1536]{1,0:T(8,128)(2,1)S(1)} %pad_maximum_fusion), channel_id=1, source_target_pairs={{0,2},{2,4},{4,6},{6,8},{8,10},{10,12},{12,14},{14,0},{1,3},{3,5},... | collective-permute-start | bytes 1179656 | tf_op jit(solution)/shard_map/ppermute | solution.py:449
  89.4 23.2 %collective-permute-start.18 = (bf16[128,1024]{1,0:T(8,128)(2,1)S(1)}, bf16[128,1024]{1,0:T(8,128)(2,1)S(1)}, u32[]{:S(2)}, u32[]{:S(2)}) collective-permute-start(bf16[128,1024]{1,0:T(8,128)(2,1)S(1)} %pad_maximum_fusion.3), channel_id=1, source_target_pairs={{0,14},{2,0},{4,2},{6,4},{8,6},{10,8},{12,10},{14,12},{1,15},{3,1}... | collective-permute-start | bytes 786440 | tf_op jit(solution)/shard_map/ppermute | solution.py:449
  100.7 14.0 %collective-permute-start.17 = (bf16[128,1024]{1,0:T(8,128)(2,1)S(1)}, bf16[128,1024]{1,0:T(8,128)(2,1)S(1)}, u32[]{:S(2)}, u32[]{:S(2)}) collective-permute-start(bf16[128,1024]{1,0:T(8,128)(2,1)S(1)} %pad_maximum_fusion.2), channel_id=1, source_target_pairs={{0,2},{2,4},{4,6},{6,8},{8,10},{10,12},{12,14},{14,0},{1,3},{3,5},... | collective-permute-start | bytes 786440 | tf_op jit(solution)/shard_map/ppermute | solution.py:449
  117.5 22.3 %all-to-all-start = ((bf16[16,20,128]{2,1,0:T(8,128)(2,1)}), bf16[16,20,128]{2,1,0:T(8,128)(2,1)S(1)}, u32[]{:S(2)}, u32[]{:S(2)}) async-start(bf16[16,20,128]{2,1,0:T(8,128)(2,1)} %get-tuple-element.103), calls=%async_computation | async-start | bytes 196608 | tf_op jit(solution)/shard_map/all_to_all | solution.py:361
  131.3 27.9 %collective-permute-start.19 = (bf16[128,768]{1,0:T(8,128)(2,1)}, bf16[128,768]{1,0:T(8,128)(2,1)S(1)}, u32[]{:S(2)}, u32[]{:S(2)}) collective-permute-start(bf16[128,768]{1,0:T(8,128)(2,1)} %get-tuple-element.101), channel_id=1, source_target_pairs={{0,1},{1,0},{2,3},{3,2},{4,5},{5,4},{6,7},{7,6},{8,9},{9,8},{10,11... | collective-permute-start | bytes 589832 | tf_op jit(solution)/shard_map/ppermute | solution.py:439
  131.5 27.7 %collective-permute-start.20 = (bf16[128,512]{1,0:T(8,128)(2,1)}, bf16[128,512]{1,0:T(8,128)(2,1)S(1)}, u32[]{:S(2)}, u32[]{:S(2)}) collective-permute-start(bf16[128,512]{1,0:T(8,128)(2,1)} %get-tuple-element.102), channel_id=1, source_target_pairs={{0,1},{1,0},{2,3},{3,2},{4,5},{5,4},{6,7},{7,6},{8,9},{9,8},{10,11... | collective-permute-start | bytes 393224 | tf_op jit(solution)/shard_map/ppermute | solution.py:439
  140.4 13.4 %all-to-all-start.1 = ((bf16[16,20,128]{2,1,0:T(8,128)(2,1)}), bf16[16,20,128]{2,1,0:T(8,128)(2,1)S(1)}, u32[]{:S(2)}, u32[]{:S(2)}) async-start(bf16[16,20,128]{2,1,0:T(8,128)(2,1)} %broadcast_in_dim.7), calls=%async_computation.1 | async-start | bytes 196608 | tf_op jit(solution)/shard_map/all_to_all | solution.py:357
  154.5 13.2 %all-to-all-start.2 = ((bf16[16,20,128]{2,1,0:T(8,128)(2,1)}), bf16[16,20,128]{2,1,0:T(8,128)(2,1)S(1)}, u32[]{:S(2)}, u32[]{:S(2)}) async-start(bf16[16,20,128]{2,1,0:T(8,128)(2,1)} %broadcast_in_dim.8), calls=%async_computation.2 | async-start | bytes 196608 | tf_op jit(solution)/shard_map/all_to_all | solution.py:357
  (7 other events, 94.9 us)

commit v2 on v1

--- a/solution.py
+++ b/solution.py
@@ -388,14 +388,23 @@
     def cross(way):
         return [(2 * i + c, 2 * ((i + way) % n) + 1 - c) for i in range(n) for c in range(2)]
 
-    a0, other_kv = pack(k_base, v_base)
-    fa = [a0, moved(a0, ahead)]
-    kb = [None, moved(other_kv, cross(-1), SEQ)]
-    b0 = lax.ppermute(other_kv, "c", swap)
-    fb = [b0, lax.ppermute(other_kv, SEQ, cross(1))]
-    ka = [a0, lax.ppermute(a0, "z", back)]
+    def halves(x):
+        return [lax.dynamic_slice_in_dim(x[0], w * half, half, 1) for w in (core, 1 - core)]
+
+    k_mine, k_other = halves(k_base)
+    fa = [moved(k_mine, ahead)]
+    kb = [moved(k_other, cross(-1), SEQ)]
+    v_mine, v_other = halves(v_base)
+    fa = [None, jnp.concatenate([fa[0], moved(v_mine, ahead)], axis=1)]
+    v_back = moved(v_other, cross(-1), SEQ)
+    kb = [None, jnp.concatenate([kb[0], v_back], axis=1)]
+    a0 = jnp.concatenate([k_mine, v_mine], axis=1)
+    other_kv = jnp.concatenate([k_other, v_other], axis=1)
+    b0 = moved(other_kv, swap, "c")
+    fb = [b0, moved(other_kv, cross(1), SEQ)]
+    ka = [a0, moved(a0, back)]
     mine_qc, other_qc = pack(base_query, cotangent)
-    qc = lax.ppermute(other_qc, "c", swap)
+    qc = moved(other_qc, swap, "c")
     tok_mine = tokens[0]
     tok_other = moved(tok_mine, swap, "c")
 

time: 169 us -> 170 us (level)
  local copies, waits for them, and re-layouts: 4.93 us -> 11.1 us
  Pallas kernels: 23.2 us -> 17.6 us
  waiting for transfers between devices: 87.4 us -> 83.5 us
  other arithmetic: 2.36 us -> 6.09 us
    ppermute x1, waiting for transfers between devices: 13 us -> 0.64 us  [shards(): kb.append(lax.ppermute(y, 'z', back))]
    ppermute x1, waiting for transfers between devices: 0.01 us -> 12.3 us  [shards(): fa.append(lax.ppermute(x, 'z', ahead))]
    ppermute x1, waiting for transfers between devices: 1 us -> 10.1 us  [shards(): kb.append(lax.ppermute(kb[1], 'z', back))]
    ppermute x9 -> x15, waiting for transfers between devices: 34.4 us -> 28.1 us  [moved(): return lax.ppermute(value, axis, pairs)]
    ppermute x1, waiting for transfers between devices: 5.91 us -> 0.01 us  [shards(): fa.append(lax.ppermute(fa[1], 'z', ahead))]
    concatenate x0 -> x2, other arithmetic: none -> 3.9 us  [the longest x1 1.95 us: shards(): other_kv = jnp.concatenate([k_other, v_other], axis=1)]
    ppermute x9 -> x15, starting transfers between devices: 15 us -> 18.4 us  [moved(): return lax.ppermute(value, axis, pairs)]
    dynamic_slice x0 -> x2, local copies, waits for them, and re-layouts: none -> 2.83 us  [halves(): lax.dynamic_slice_in_dim(x[0], w * half, half, 1)]
  transfers between devices with their start and end apart: 24 -> 26, of which waited for: 14 -> 16; matrix products, arithmetic and copies ran while one was open for 3% -> 9% of each run, Pallas kernels for 12% -> 8%
where the time goes in v2:
time: 170 us; the launch traced here: 169 us
  waiting for transfers between devices  83.5 us (49%)
  starting transfers between devices  50.2 us (30%)
  Pallas kernels  17.6 us (10%)
  local copies, waits for them, and re-layouts  11.1 us (7%)
  other arithmetic  6.09 us (4%)
    ppermute x15, waiting for transfers between devices, moved(): return lax.ppermute(value, axis, pairs)  28.1 us
    ppermute x15, starting transfers between devices, moved(): return lax.ppermute(value, axis, pairs)  18.4 us
    all_to_all x2, waiting for transfers between devices, sent(): return lax.all_to_all(copies, axis, 0, 0, tiled=True)  13.1 us
    all_to_all x1, starting transfers between devices, total_of(): lax.all_to_all(blocks, SEQ, 0, 0, tiled=True).astype(f32).sum(axis=0)  12.9 us
    ppermute x1, waiting for transfers between devices, shards(): fa.append(lax.ppermute(x, 'z', ahead))  12.3 us
    pallas_call x6, Pallas kernels, attend(): pl.pallas_call(functools.partial(attend_body, kind=kind, reach=reach, hea...  11.9 us
    all_to_all x2, starting transfers between devices, sent(): return lax.all_to_all(copies, axis, 0, 0, tiled=True)  11.4 us
    ppermute x1, waiting for transfers between devices, shards(): fb.append(lax.ppermute(x, 'z', ahead))  10.7 us
  transfers between devices with their start and end apart: 26, of which 16 were waited for; matrix products, arithmetic and copies ran while one was open for 9% of the time, Pallas kernels for 8%

profile of v2, /device:TPU:1, one launch (start us, length us, event | category | flops | bytes accessed | tf_op | source)
XLA Modules:
  0.0 169.4 jit_solution(4292337770819572147)
XLA Ops:
  0.7 3.3 %collective-permute-start.8 = (bf16[128,5120]{1,0:T(8,128)(2,1)}, bf16[128,5120]{1,0:T(8,128)(2,1)S(1)}, u32[]{:S(2)}, u32[]{:S(2)}) collective-permute-start(bf16[128,5120]{1,0:T(8,128)(2,1)} %bitcast.15), channel_id=1, source_target_pairs={{0,1},{1,0},{2,3},{3,2},{4,5},{5,4},{6,7},{7,6},{8,9},{9,8},{10,11... | collective-permute-start | bytes 3932168 | tf_op jit(solution)/shard_map/ppermute | solution.py:458
  5.9 4.0 %collective-permute-start.3 = (bf16[128,1280]{1,0:T(8,128)(2,1)}, bf16[128,1280]{1,0:T(8,128)(2,1)}, u32[]{:S(2)}, u32[]{:S(2)}) collective-permute-start(bf16[128,1280]{1,0:T(8,128)(2,1)} %get-tuple-element.110), channel_id=1, source_target_pairs={{0,15},{1,14},{2,1},{3,0},{4,3},{5,2},{6,5},{7,4},{8,7},{9,6},{10,... | collective-permute-start | bytes 983048 | tf_op jit(solution)/shard_map/ppermute | solution.py:458
  16.4 2.1 %pack.1 = (bf16[128,2560]{1,0:T(8,128)(2,1)}, bf16[128,2560]{1,0:T(8,128)(2,1)}) custom-call(bf16[1,128,2560]{2,1,0:T(8,128)(2,1)} %a.1, bf16[1,128,2560]{2,1,0:T(8,128)(2,1)} %b.1), custom_call_target="tpu_custom_call" | custom-call | flops 2000000 | bytes 5000000 | tf_op jit(solution)/shard_map/pack/pallas_call | solution.py:63
  25.1 4.2 %collective-permute-done.1 = bf16[128,1280]{1,0:T(8,128)(2,1)} collective-permute-done((bf16[128,1280]{1,0:T(8,128)(2,1)}, bf16[128,1280]{1,0:T(8,128)(2,1)}, u32[]{:S(2)}, u32[]{:S(2)}) %collective-permute-start.1) | collective-permute-done | bytes 327712 | tf_op jit(solution)/shard_map/ppermute | solution.py:458
  34.8 2.9 %query.1 = (bf16[256,1280]{1,0:T(8,128)(2,1)S(1)}, bf16[256,256]{1,0:T(8,128)(2,1)S(1)}, f32[8,256]{1,0:T(8,128)S(1)}, bf16[128,5120]{1,0:T(8,128)(2,1)S(1)}) custom-call(bf16[128,5120]{1,0:T(8,128)(2,1)S(1)} %bitcast.16, bf16[128,5120]{1,0:T(8,128)(2,1)S(1)} %collective-permute-done.8.tok_other, bf16[5120,256]{1,0:T(8,128)(2,1)S(1)} %copy-done.2, ...), custom_call_target="tpu_custom_call" | custom-call | flops 838860800 | bytes 8000000 | tf_op jit(solution)/shard_map/query/pallas_call | solution.py:109
  37.7 4.3 %shard_map.95 = (f32[8,128]{1,0:T(8,128)S(1)}, f32[256,1280]{1,0:T(8,128)S(1)}, f32[256,1280]{1,0:T(8,128)S(1)}, f32[256,1280]{1,0:T(8,128)S(1)}, f32[256,1280]{...) custom-call(s32[2]{0:T(128)S(1)} %pad_add_fusion.refs_0_, f32[8,128]{1,0:T(8,128)S(1)} %broadcast_in_dim.6.refs_1_, ...), custom_call_target="tpu_custom_call" | custom-call | flops 1677721600 | bytes 8000000 | tf_op jit(solution)/shard_map/pallas_call | solution.py:342
  42.0 2.1 %collective-permute-done.6.refs_6_ = bf16[128,2560]{1,0:T(8,128)(2,1)S(1)} collective-permute-done((bf16[128,2560]{1,0:T(8,128)(2,1)}, bf16[128,2560]{1,0:T(8,128)(2,1)S(1)}, u32[]{:S(2)}, u32[]{:S(2)}) %collective-permute-start.6) | collective-permute-done | bytes 655392 | tf_op jit(solution)/shard_map/ppermute | solution.py:458
  44.1 2.7 %collective-permute-start.14 = (bf16[128,2560]{1,0:T(8,128)(2,1)S(1)}, bf16[128,2560]{1,0:T(8,128)(2,1)S(1)}, u32[]{:S(2)}, u32[]{:S(2)}) collective-permute-start(bf16[128,2560]{1,0:T(8,128)(2,1)S(1)} %collective-permute-done.7.refs_7_), channel_id=1, source_target_pairs={{0,14},{2,0},{4,2},{6,4},{8,6},{10,8},{12,10},{14,12},{1,15},{3,1}... | collective-permute-start | bytes 1966088 | tf_op jit(solution)/shard_map/ppermute | solution.py:423
  47.9 10.1 %collective-permute-done.5.refs_8_ = bf16[128,2560]{1,0:T(8,128)(2,1)S(1)} collective-permute-done((bf16[128,2560]{1,0:T(8,128)(2,1)S(1)}, bf16[128,2560]{1,0:T(8,128)(2,1)S(1)}, u32[]{:S(2)}, u32[]{:S(2)}) %collective-permute-start.5) | collective-permute-done | bytes 655392 | tf_op jit(solution)/shard_map/ppermute | solution.py:418
  58.0 2.7 %collective-permute-start.12 = (bf16[128,2560]{1,0:T(8,128)(2,1)S(1)}, bf16[128,2560]{1,0:T(8,128)(2,1)S(1)}, u32[]{:S(2)}, u32[]{:S(2)}) collective-permute-start(bf16[128,2560]{1,0:T(8,128)(2,1)S(1)} %collective-permute-done.5.refs_8_), channel_id=1, source_target_pairs={{0,14},{2,0},{4,2},{6,4},{8,6},{10,8},{12,10},{14,12},{1,15},{3,1}... | collective-permute-start | bytes 1966088 | tf_op jit(solution)/shard_map/ppermute | solution.py:432
  60.7 10.7 %collective-permute-done.13.refs_6_ = bf16[128,2560]{1,0:T(8,128)(2,1)S(1)} collective-permute-done((bf16[128,2560]{1,0:T(8,128)(2,1)S(1)}, bf16[128,2560]{1,0:T(8,128)(2,1)S(1)}, u32[]{:S(2)}, u32[]{:S(2)}) %collective-permute-start.13) | collective-permute-done | bytes 655392 | tf_op jit(solution)/shard_map/ppermute | solution.py:422
  73.1 12.3 %collective-permute-done.11.refs_5_ = bf16[128,2560]{1,0:T(8,128)(2,1)S(1)} collective-permute-done((bf16[128,2560]{1,0:T(8,128)(2,1)S(1)}, bf16[128,2560]{1,0:T(8,128)(2,1)S(1)}, u32[]{:S(2)}, u32[]{:S(2)}) %collective-permute-start.11) | collective-permute-done | bytes 655392 | tf_op jit(solution)/shard_map/ppermute | solution.py:431
  87.8 2.7 %collective-permute-start.16 = (bf16[128,2560]{1,0:T(8,128)(2,1)S(1)}, bf16[128,2560]{1,0:T(8,128)(2,1)S(1)}, u32[]{:S(2)}, u32[]{:S(2)}) collective-permute-start(bf16[128,2560]{1,0:T(8,128)(2,1)S(1)} %collective-permute-done.14.refs_7_), channel_id=1, source_target_pairs={{0,14},{2,0},{4,2},{6,4},{8,6},{10,8},{12,10},{14,12},{1,15},{3,1}... | collective-permute-start | bytes 1966088 | tf_op jit(solution)/shard_map/ppermute | solution.py:458
  90.6 2.7 %collective-permute-start.20 = (bf16[128,1024]{1,0:T(8,128)(2,1)S(1)}, bf16[128,1024]{1,0:T(8,128)(2,1)S(1)}, u32[]{:S(2)}, u32[]{:S(2)}) collective-permute-start(bf16[128,1024]{1,0:T(8,128)(2,1)S(1)} %pad_maximum_fusion.5), channel_id=1, source_target_pairs={{0,14},{2,0},{4,2},{6,4},{8,6},{10,8},{12,10},{14,12},{1,15},{3,1}... | collective-permute-start | bytes 786440 | tf_op jit(solution)/shard_map/ppermute | solution.py:458
  93.4 9.4 %collective-permute-done.15.refs_6_ = bf16[128,2560]{1,0:T(8,128)(2,1)S(1)} collective-permute-done((bf16[128,2560]{1,0:T(8,128)(2,1)S(1)}, bf16[128,2560]{1,0:T(8,128)(2,1)S(1)}, u32[]{:S(2)}, u32[]{:S(2)}) %collective-permute-start.15) | collective-permute-done | bytes 655392 | tf_op jit(solution)/shard_map/ppermute | solution.py:458
  102.8 5.7 %collective-permute-done.16.refs_7_ = bf16[128,2560]{1,0:T(8,128)(2,1)S(1)} collective-permute-done((bf16[128,2560]{1,0:T(8,128)(2,1)S(1)}, bf16[128,2560]{1,0:T(8,128)(2,1)S(1)}, u32[]{:S(2)}, u32[]{:S(2)}) %collective-permute-start.16) | collective-permute-done | bytes 655392 | tf_op jit(solution)/shard_map/ppermute | solution.py:458
  114.1 2.7 %collective-permute-done.19.refs_5_ = bf16[128,1024]{1,0:T(8,128)(2,1)S(1)} collective-permute-done((bf16[128,1024]{1,0:T(8,128)(2,1)S(1)}, bf16[128,1024]{1,0:T(8,128)(2,1)S(1)}, u32[]{:S(2)}, u32[]{:S(2)}) %collective-permute-start.19) | collective-permute-done | bytes 262176 | tf_op jit(solution)/shard_map/ppermute | solution.py:458
  116.9 2.7 %shard_map.100 = (bf16[128,512]{1,0:T(8,128)(2,1)}, bf16[128,512]{1,0:T(8,128)(2,1)}, bf16[16,20,128]{2,1,0:T(8,128)(2,1)}) custom-call(s32[2]{0:T(128)S(1)} %pad_add_fusion.refs_0_, f32[8,128]{1,0:T(8,128)S(1)} %get-tuple-element.82.refs_1_, bf16[256,1280]{1,0:T(8,128)(2,1)S(1)} %get-tuple-element.53.refs_2_, bf16[128,1280]{1,0:T(8,128)(2,1)S(1)} %slice.27.refs_3_, ...), custom_call_target="tpu_custom_call" | custom-call | flops 671088640 | bytes 8000000 | tf_op jit(solution)/shard_map/pallas_call | solution.py:342
  119.6 12.9 %all-to-all-start = ((bf16[16,20,128]{2,1,0:T(8,128)(2,1)}), bf16[16,20,128]{2,1,0:T(8,128)(2,1)S(1)}, u32[]{:S(2)}, u32[]{:S(2)}) async-start(bf16[16,20,128]{2,1,0:T(8,128)(2,1)} %get-tuple-element.99), calls=%async_computation | async-start | bytes 196608 | tf_op jit(solution)/shard_map/all_to_all | solution.py:361
  133.0 7.9 %all-to-all-done = bf16[16,20,128]{2,1,0:T(8,128)(2,1)S(1)} async-done(((bf16[16,20,128]{2,1,0:T(8,128)(2,1)}), bf16[16,20,128]{2,1,0:T(8,128)(2,1)S(1)}, u32[]{:S(2)}, u32[]{:S(2)}) %all-to-all-start) | async-done | bytes 81952 | tf_op jit(solution)/shard_map/all_to_all | solution.py:361
  141.5 6.8 %all-to-all-start.1 = ((bf16[16,20,128]{2,1,0:T(8,128)(2,1)}), bf16[16,20,128]{2,1,0:T(8,128)(2,1)S(1)}, u32[]{:S(2)}, u32[]{:S(2)}) async-start(bf16[16,20,128]{2,1,0:T(8,128)(2,1)} %broadcast_in_dim.7), calls=%async_computation.1 | async-start | bytes 196608 | tf_op jit(solution)/shard_map/all_to_all | solution.py:357
  148.3 6.6 %all-to-all-done.1 = bf16[16,20,128]{2,1,0:T(8,128)(2,1)S(1)} async-done(((bf16[16,20,128]{2,1,0:T(8,128)(2,1)}), bf16[16,20,128]{2,1,0:T(8,128)(2,1)S(1)}, u32[]{:S(2)}, u32[]{:S(2)}) %all-to-all-start.1) | async-done | bytes 81952 | tf_op jit(solution)/shard_map/all_to_all | solution.py:357
  155.6 4.7 %all-to-all-start.2 = ((bf16[16,20,128]{2,1,0:T(8,128)(2,1)}), bf16[16,20,128]{2,1,0:T(8,128)(2,1)S(1)}, u32[]{:S(2)}, u32[]{:S(2)}) async-start(bf16[16,20,128]{2,1,0:T(8,128)(2,1)} %broadcast_in_dim.8), calls=%async_computation.2 | async-start | bytes 196608 | tf_op jit(solution)/shard_map/all_to_all | solution.py:357
  162.3 6.5 %all-to-all-done.2.blocks = bf16[16,20,128]{2,1,0:T(8,128)(2,1)S(1)} async-done(((bf16[16,20,128]{2,1,0:T(8,128)(2,1)}), bf16[16,20,128]{2,1,0:T(8,128)(2,1)S(1)}, u32[]{:S(2)}, u32[]{:S(2)}) %all-to-all-start.2) | async-done | bytes 81952 | tf_op jit(solution)/shard_map/all_to_all | solution.py:357
  (78 shorter events, 35.9 us)
Async XLA Ops:
  0.7 30.9 %collective-permute-start.8 = (bf16[128,5120]{1,0:T(8,128)(2,1)}, bf16[128,5120]{1,0:T(8,128)(2,1)S(1)}, u32[]{:S(2)}, u32[]{:S(2)}) collective-permute-start(bf16[128,5120]{1,0:T(8,128)(2,1)} %bitcast.15), channel_id=1, source_target_pairs={{0,1},{1,0},{2,3},{3,2},{4,5},{5,4},{6,7},{7,6},{8,9},{9,8},{10,11... | collective-permute-start | bytes 3932168 | tf_op jit(solution)/shard_map/ppermute | solution.py:458
  5.9 13.7 %collective-permute-start.3 = (bf16[128,1280]{1,0:T(8,128)(2,1)}, bf16[128,1280]{1,0:T(8,128)(2,1)}, u32[]{:S(2)}, u32[]{:S(2)}) collective-permute-start(bf16[128,1280]{1,0:T(8,128)(2,1)} %get-tuple-element.110), channel_id=1, source_target_pairs={{0,15},{1,14},{2,1},{3,0},{4,3},{5,2},{6,5},{7,4},{8,7},{9,6},{10,... | collective-permute-start | bytes 983048 | tf_op jit(solution)/shard_map/ppermute | solution.py:458
  10.7 14.2 %collective-permute-start.4 = (bf16[128,1280]{1,0:T(8,128)(2,1)}, bf16[128,1280]{1,0:T(8,128)(2,1)}, u32[]{:S(2)}, u32[]{:S(2)}) collective-permute-start(bf16[128,1280]{1,0:T(8,128)(2,1)} %get-tuple-element.108), channel_id=1, source_target_pairs={{0,15},{1,14},{2,1},{3,0},{4,3},{5,2},{6,5},{7,4},{8,7},{9,6},{10,... | collective-permute-start | bytes 983048 | tf_op jit(solution)/shard_map/ppermute | solution.py:458
  12.4 16.9 %collective-permute-start.1 = (bf16[128,1280]{1,0:T(8,128)(2,1)}, bf16[128,1280]{1,0:T(8,128)(2,1)}, u32[]{:S(2)}, u32[]{:S(2)}) collective-permute-start(bf16[128,1280]{1,0:T(8,128)(2,1)} %get-tuple-element.109), channel_id=1, source_target_pairs={{0,2},{2,4},{4,6},{6,8},{8,10},{10,12},{12,14},{14,0},{1,3},{3,5},... | collective-permute-start | bytes 983048 | tf_op jit(solution)/shard_map/ppermute | solution.py:458
  19.6 18.1 %collective-permute-start.10 = (bf16[128,2560]{1,0:T(8,128)(2,1)}, bf16[128,2560]{1,0:T(8,128)(2,1)S(1)}, u32[]{:S(2)}, u32[]{:S(2)}) collective-permute-start(bf16[128,2560]{1,0:T(8,128)(2,1)} %pad_maximum_fusion), channel_id=1, source_target_pairs={{0,1},{1,0},{2,3},{3,2},{4,5},{5,4},{6,7},{7,6},{8,9},{9,8},{10,11... | collective-permute-start | bytes 1966088 | tf_op jit(solution)/shard_map/ppermute | solution.py:458
  25.0 19.1 %collective-permute-start.6 = (bf16[128,2560]{1,0:T(8,128)(2,1)}, bf16[128,2560]{1,0:T(8,128)(2,1)S(1)}, u32[]{:S(2)}, u32[]{:S(2)}) collective-permute-start(bf16[128,2560]{1,0:T(8,128)(2,1)} %pad_maximum_fusion), channel_id=1, source_target_pairs={{0,3},{1,2},{2,5},{3,4},{4,7},{5,6},{6,9},{7,8},{8,11},{9,10},{10,... | collective-permute-start | bytes 1966088 | tf_op jit(solution)/shard_map/ppermute | solution.py:458
  29.3 14.9 %collective-permute-start.7 = (bf16[128,2560]{1,0:T(8,128)(2,1)S(1)}, bf16[128,2560]{1,0:T(8,128)(2,1)S(1)}, u32[]{:S(2)}, u32[]{:S(2)}) collective-permute-start(bf16[128,2560]{1,0:T(8,128)(2,1)S(1)} %copy-done.4), channel_id=1, source_target_pairs={{0,14},{2,0},{4,2},{6,4},{8,6},{10,8},{12,10},{14,12},{1,15},{3,1}... | collective-permute-start | bytes 1966088 | tf_op jit(solution)/shard_map/ppermute | solution.py:458
  31.3 26.7 %collective-permute-start.5 = (bf16[128,2560]{1,0:T(8,128)(2,1)S(1)}, bf16[128,2560]{1,0:T(8,128)(2,1)S(1)}, u32[]{:S(2)}, u32[]{:S(2)}) collective-permute-start(bf16[128,2560]{1,0:T(8,128)(2,1)S(1)} %constant_dynamic-update-slice_fusion.2.refs_8_), channel_id=1, source_target_pairs={{0,14},{2,0},{4,2},{6,4},{8,6},{10,8},{12,10},{14,12},{1,15},{3,1}... | collective-permute-start | bytes 1966088 | tf_op jit(solution)/shard_map/ppermute | solution.py:418
  31.6 26.4 %collective-permute-start.2 = (bf16[128,2560]{1,0:T(8,128)(2,1)S(1)}, bf16[128,2560]{1,0:T(8,128)(2,1)S(1)}, u32[]{:S(2)}, u32[]{:S(2)}) collective-permute-start(bf16[128,2560]{1,0:T(8,128)(2,1)S(1)} %constant_dynamic-update-slice_fusion.refs_5_), channel_id=1, source_target_pairs={{0,2},{2,4},{4,6},{6,8},{8,10},{10,12},{12,14},{14,0},{1,3},{3,5},... | collective-permute-start | bytes 1966088 | tf_op jit(solution)/shard_map/ppermute | solution.py:417
  44.1 27.3 %collective-permute-start.13 = (bf16[128,2560]{1,0:T(8,128)(2,1)S(1)}, bf16[128,2560]{1,0:T(8,128)(2,1)S(1)}, u32[]{:S(2)}, u32[]{:S(2)}) collective-permute-start(bf16[128,2560]{1,0:T(8,128)(2,1)S(1)} %collective-permute-done.6.refs_6_), channel_id=1, source_target_pairs={{0,2},{2,4},{4,6},{6,8},{8,10},{10,12},{12,14},{14,0},{1,3},{3,5},... | collective-permute-start | bytes 1966088 | tf_op jit(solution)/shard_map/ppermute | solution.py:422
  44.1 27.9 %collective-permute-start.14 = (bf16[128,2560]{1,0:T(8,128)(2,1)S(1)}, bf16[128,2560]{1,0:T(8,128)(2,1)S(1)}, u32[]{:S(2)}, u32[]{:S(2)}) collective-permute-start(bf16[128,2560]{1,0:T(8,128)(2,1)S(1)} %collective-permute-done.7.refs_7_), channel_id=1, source_target_pairs={{0,14},{2,0},{4,2},{6,4},{8,6},{10,8},{12,10},{14,12},{1,15},{3,1}... | collective-permute-start | bytes 1966088 | tf_op jit(solution)/shard_map/ppermute | solution.py:423
  58.0 27.4 %collective-permute-start.11 = (bf16[128,2560]{1,0:T(8,128)(2,1)S(1)}, bf16[128,2560]{1,0:T(8,128)(2,1)S(1)}, u32[]{:S(2)}, u32[]{:S(2)}) collective-permute-start(bf16[128,2560]{1,0:T(8,128)(2,1)S(1)} %collective-permute-done.2.refs_5_), channel_id=1, source_target_pairs={{0,2},{2,4},{4,6},{6,8},{8,10},{10,12},{12,14},{14,0},{1,3},{3,5},... | collective-permute-start | bytes 1966088 | tf_op jit(solution)/shard_map/ppermute | solution.py:431
  58.0 28.1 %collective-permute-start.12 = (bf16[128,2560]{1,0:T(8,128)(2,1)S(1)}, bf16[128,2560]{1,0:T(8,128)(2,1)S(1)}, u32[]{:S(2)}, u32[]{:S(2)}) collective-permute-start(bf16[128,2560]{1,0:T(8,128)(2,1)S(1)} %collective-permute-done.5.refs_8_), channel_id=1, source_target_pairs={{0,14},{2,0},{4,2},{6,4},{8,6},{10,8},{12,10},{14,12},{1,15},{3,1}... | collective-permute-start | bytes 1966088 | tf_op jit(solution)/shard_map/ppermute | solution.py:432
  86.2 23.6 %collective-permute-start.18 = (bf16[128,1536]{1,0:T(8,128)(2,1)S(1)}, bf16[128,1536]{1,0:T(8,128)(2,1)S(1)}, u32[]{:S(2)}, u32[]{:S(2)}) collective-permute-start(bf16[128,1536]{1,0:T(8,128)(2,1)S(1)} %pad_maximum_fusion.3), channel_id=1, source_target_pairs={{0,14},{2,0},{4,2},{6,4},{8,6},{10,8},{12,10},{14,12},{1,15},{3,1}... | collective-permute-start | bytes 1179656 | tf_op jit(solution)/shard_map/ppermute | solution.py:458
  87.8 15.0 %collective-permute-start.15 = (bf16[128,2560]{1,0:T(8,128)(2,1)S(1)}, bf16[128,2560]{1,0:T(8,128)(2,1)S(1)}, u32[]{:S(2)}, u32[]{:S(2)}) collective-permute-start(bf16[128,2560]{1,0:T(8,128)(2,1)S(1)} %collective-permute-done.13.refs_6_), channel_id=1, source_target_pairs={{0,2},{2,4},{4,6},{6,8},{8,10},{10,12},{12,14},{14,0},{1,3},{3,5},... | collective-permute-start | bytes 1966088 | tf_op jit(solution)/shard_map/ppermute | solution.py:458
  87.8 20.8 %collective-permute-start.16 = (bf16[128,2560]{1,0:T(8,128)(2,1)S(1)}, bf16[128,2560]{1,0:T(8,128)(2,1)S(1)}, u32[]{:S(2)}, u32[]{:S(2)}) collective-permute-start(bf16[128,2560]{1,0:T(8,128)(2,1)S(1)} %collective-permute-done.14.refs_7_), channel_id=1, source_target_pairs={{0,14},{2,0},{4,2},{6,4},{8,6},{10,8},{12,10},{14,12},{1,15},{3,1}... | collective-permute-start | bytes 1966088 | tf_op jit(solution)/shard_map/ppermute | solution.py:458
  90.5 20.8 %collective-permute-start.17 = (bf16[128,1536]{1,0:T(8,128)(2,1)S(1)}, bf16[128,1536]{1,0:T(8,128)(2,1)S(1)}, u32[]{:S(2)}, u32[]{:S(2)}) collective-permute-start(bf16[128,1536]{1,0:T(8,128)(2,1)S(1)} %pad_maximum_fusion.2), channel_id=1, source_target_pairs={{0,2},{2,4},{4,6},{6,8},{8,10},{10,12},{12,14},{14,0},{1,3},{3,5},... | collective-permute-start | bytes 1179656 | tf_op jit(solution)/shard_map/ppermute | solution.py:458
  90.6 23.5 %collective-permute-start.20 = (bf16[128,1024]{1,0:T(8,128)(2,1)S(1)}, bf16[128,1024]{1,0:T(8,128)(2,1)S(1)}, u32[]{:S(2)}, u32[]{:S(2)}) collective-permute-start(bf16[128,1024]{1,0:T(8,128)(2,1)S(1)} %pad_maximum_fusion.5), channel_id=1, source_target_pairs={{0,14},{2,0},{4,2},{6,4},{8,6},{10,8},{12,10},{14,12},{1,15},{3,1}... | collective-permute-start | bytes 786440 | tf_op jit(solution)/shard_map/ppermute | solution.py:458
  102.8 14.0 %collective-permute-start.19 = (bf16[128,1024]{1,0:T(8,128)(2,1)S(1)}, bf16[128,1024]{1,0:T(8,128)(2,1)S(1)}, u32[]{:S(2)}, u32[]{:S(2)}) collective-permute-start(bf16[128,1024]{1,0:T(8,128)(2,1)S(1)} %pad_maximum_fusion.4), channel_id=1, source_target_pairs={{0,2},{2,4},{4,6},{6,8},{8,10},{10,12},{12,14},{14,0},{1,3},{3,5},... | collective-permute-start | bytes 786440 | tf_op jit(solution)/shard_map/ppermute | solution.py:458
  119.6 21.3 %all-to-all-start = ((bf16[16,20,128]{2,1,0:T(8,128)(2,1)}), bf16[16,20,128]{2,1,0:T(8,128)(2,1)S(1)}, u32[]{:S(2)}, u32[]{:S(2)}) async-start(bf16[16,20,128]{2,1,0:T(8,128)(2,1)} %get-tuple-element.99), calls=%async_computation | async-start | bytes 196608 | tf_op jit(solution)/shard_map/all_to_all | solution.py:361
  132.4 27.8 %collective-permute-start.21 = (bf16[128,768]{1,0:T(8,128)(2,1)S(1)}, bf16[128,768]{1,0:T(8,128)(2,1)S(1)}, u32[]{:S(2)}, u32[]{:S(2)}) collective-permute-start(bf16[128,768]{1,0:T(8,128)(2,1)S(1)} %copy-done.8), channel_id=1, source_target_pairs={{0,1},{1,0},{2,3},{3,2},{4,5},{5,4},{6,7},{7,6},{8,9},{9,8},{10,11... | collective-permute-start | bytes 589832 | tf_op jit(solution)/shard_map/ppermute | solution.py:448
  132.6 27.6 %collective-permute-start.22 = (bf16[128,512]{1,0:T(8,128)(2,1)}, bf16[128,512]{1,0:T(8,128)(2,1)S(1)}, u32[]{:S(2)}, u32[]{:S(2)}) collective-permute-start(bf16[128,512]{1,0:T(8,128)(2,1)} %get-tuple-element.98), channel_id=1, source_target_pairs={{0,1},{1,0},{2,3},{3,2},{4,5},{5,4},{6,7},{7,6},{8,9},{9,8},{10,11... | collective-permute-start | bytes 393224 | tf_op jit(solution)/shard_map/ppermute | solution.py:448
  141.5 13.4 %all-to-all-start.1 = ((bf16[16,20,128]{2,1,0:T(8,128)(2,1)}), bf16[16,20,128]{2,1,0:T(8,128)(2,1)S(1)}, u32[]{:S(2)}, u32[]{:S(2)}) async-start(bf16[16,20,128]{2,1,0:T(8,128)(2,1)} %broadcast_in_dim.7), calls=%async_computation.1 | async-start | bytes 196608 | tf_op jit(solution)/shard_map/all_to_all | solution.py:357
  155.6 13.2 %all-to-all-start.2 = ((bf16[16,20,128]{2,1,0:T(8,128)(2,1)}), bf16[16,20,128]{2,1,0:T(8,128)(2,1)S(1)}, u32[]{:S(2)}, u32[]{:S(2)}) async-start(bf16[16,20,128]{2,1,0:T(8,128)(2,1)} %broadcast_in_dim.8), calls=%async_computation.2 | async-start | bytes 196608 | tf_op jit(solution)/shard_map/all_to_all | solution.py:357
  (11 other events, 156.3 us)

commit v3 on v2

--- a/solution.py
+++ b/solution.py
@@ -32,6 +32,45 @@
     return lax.dot_general(
         a, b, (((1,), (1,)), ((), ())), precision=precision, preferred_element_type=f32
     )
+
+
+def halve_body(a, mine, other, held, came, went):
+    half = a.shape[2] // CORES
+    core = lax.axis_index("c")
+    pairs = []
+    for i, (out, which) in enumerate(((mine, core), (other, 1 - core))):
+        columns = pl.ds(pl.multiple_of(which * half, HEAD_DIM), half)
+        pairs.append(
+            (
+                pltpu.make_async_copy(a.at[0, :, columns], held.at[i], came.at[i]),
+                pltpu.make_async_copy(held.at[i], out, went.at[i]),
+            )
+        )
+    for come, _ in pairs:
+        come.start()
+    for come, go in pairs:
+        come.wait()
+        go.start()
+    for _, go in pairs:
+        go.wait()
+
+
+def halve(a):
+    _, rows, width = a.shape
+    half = width // CORES
+    return pl.pallas_call(
+        halve_body,
+        in_specs=[pl.BlockSpec(memory_space=pl.ANY)],
+        out_specs=[pl.BlockSpec(memory_space=pl.ANY)] * 2,
+        out_shape=[pltpu.HBM((rows, half), a.dtype)] * 2,
+        scratch_shapes=[
+            pltpu.VMEM((CORES, rows, half), a.dtype),
+            pltpu.SemaphoreType.DMA((CORES,)),
+            pltpu.SemaphoreType.DMA((CORES,)),
+        ],
+        name="halve",
+        cost_estimate=pl.CostEstimate(flops=1_000_000, bytes_accessed=2_600_000, transcendentals=0),
+    )(a)
 
 
 def pack_body(a, b, mine, other, held, came, went):
@@ -388,13 +427,10 @@
     def cross(way):
         return [(2 * i + c, 2 * ((i + way) % n) + 1 - c) for i in range(n) for c in range(2)]
 
-    def halves(x):
-        return [lax.dynamic_slice_in_dim(x[0], w * half, half, 1) for w in (core, 1 - core)]
-
-    k_mine, k_other = halves(k_base)
+    k_mine, k_other = halve(k_base)
     fa = [moved(k_mine, ahead)]
     kb = [moved(k_other, cross(-1), SEQ)]
-    v_mine, v_other = halves(v_base)
+    v_mine, v_other = halve(v_base)
     fa = [None, jnp.concatenate([fa[0], moved(v_mine, ahead)], axis=1)]
     v_back = moved(v_other, cross(-1), SEQ)
     kb = [None, jnp.concatenate([kb[0], v_back], axis=1)]
@@ -435,7 +471,7 @@
             ka.append(moved(ka[d + 1], back))
     parts = []
     heads = half // HEAD_DIM
-    split = heads // 2 + heads % 4 // 2
+    split = heads - max(1, 3 * heads // 10)
     for start, stop in ((0, split), (split, heads)):
         cut = [head_part(p, start, stop) for p in (x, y)]
         parts.append((moved(cut[0], ahead), moved(cut[1], back)))

time: 170 us -> 173 us (1.018)
  waiting for transfers between devices: 83.5 us -> 78.9 us
  Pallas kernels: 17.6 us -> 21.9 us
  other arithmetic: 6.09 us -> 2.19 us
  starting transfers between devices: 50.2 us -> 54 us
  local copies, waits for them, and re-layouts: 11.1 us -> 14.3 us
    ppermute x1, waiting for transfers between devices: 0.01 us -> 9.16 us  [shards(): fa.append(lax.ppermute(fa[1], 'z', ahead))]
    ppermute x1, waiting for transfers between devices: 10.1 us -> 1.14 us  [shards(): kb.append(lax.ppermute(kb[1], 'z', back))]
    ppermute x15, waiting for transfers between devices: 28.1 us -> 23.7 us  [moved(): return lax.ppermute(value, axis, pairs)]
    concatenate x2 -> x0, other arithmetic: 3.9 us -> none  [the longest x1 1.95 us: shards(): other_kv = jnp.concatenate([k_other, v_other], axis=1)]
    pallas_call x0 -> x2, Pallas kernels: none -> 3.68 us  [halve(): pl.pallas_call(halve_body, in_specs=[pl.BlockSpec(memory_space=pl.ANY)],...]
    concatenate x0 -> x2, local copies, waits for them, and re-layouts: none -> 3.46 us  [the longest x1 1.75 us: shards(): other_kv = jnp.concatenate([k_other, v_other], axis=1)]
    ppermute x15, starting transfers between devices: 18.4 us -> 21.4 us  [moved(): return lax.ppermute(value, axis, pairs)]
    dynamic_slice x2 -> x0, local copies, waits for them, and re-layouts: 2.83 us -> none  [halves(): lax.dynamic_slice_in_dim(x[0], w * half, half, 1)]
  transfers between devices with their start and end apart: 26 -> 26, of which waited for: 16 -> 15; matrix products, arithmetic and copies ran while one was open for 9% -> 8% of each run, Pallas kernels for 8% -> 11%
where the time goes in v3:
time: 173 us; the launch traced here: 172 us
  waiting for transfers between devices  78.9 us (46%)
  starting transfers between devices  54 us (31%)
  Pallas kernels  21.9 us (13%)
  local copies, waits for them, and re-layouts  14.3 us (8%)
  other arithmetic  2.19 us (1%)
    ppermute x15, waiting for transfers between devices, moved(): return lax.ppermute(value, axis, pairs)  23.7 us
    ppermute x15, starting transfers between devices, moved(): return lax.ppermute(value, axis, pairs)  21.4 us
    all_to_all x2, waiting for transfers between devices, sent(): return lax.all_to_all(copies, axis, 0, 0, tiled=True)  13.1 us
    all_to_all x1, starting transfers between devices, total_of(): lax.all_to_all(blocks, SEQ, 0, 0, tiled=True).astype(f32).sum(axis=0)  12.5 us
    pallas_call x6, Pallas kernels, attend(): pl.pallas_call(functools.partial(attend_body, kind=kind, reach=reach, hea...  12.5 us
    ppermute x1, waiting for transfers between devices, shards(): fa.append(lax.ppermute(x, 'z', ahead))  11.8 us
    all_to_all x2, starting transfers between devices, sent(): return lax.all_to_all(copies, axis, 0, 0, tiled=True)  11.4 us
    ppermute x1, waiting for transfers between devices, shards(): fb.append(lax.ppermute(x, 'z', ahead))  10.2 us
  transfers between devices with their start and end apart: 26, of which 15 were waited for; matrix products, arithmetic and copies ran while one was open for 8% of the time, Pallas kernels for 11%

profile of v3, /device:TPU:1, one launch (start us, length us, event | category | flops | bytes accessed | tf_op | source)
XLA Modules:
  0.0 172.3 jit_solution(8117188743927091152)
XLA Ops:
  0.6 3.3 %collective-permute-start.8 = (bf16[128,5120]{1,0:T(8,128)(2,1)}, bf16[128,5120]{1,0:T(8,128)(2,1)S(1)}, u32[]{:S(2)}, u32[]{:S(2)}) collective-permute-start(bf16[128,5120]{1,0:T(8,128)(2,1)} %bitcast.7), channel_id=1, source_target_pairs={{0,1},{1,0},{2,3},{3,2},{4,5},{5,4},{6,7},{7,6},{8,9},{9,8},{10,11... | collective-permute-start | bytes 3932168 | tf_op jit(solution)/shard_map/ppermute | solution.py:494
  9.3 2.4 %collective-permute-start.3 = (bf16[128,1280]{1,0:T(8,128)(2,1)}, bf16[128,1280]{1,0:T(8,128)(2,1)}, u32[]{:S(2)}, u32[]{:S(2)}) collective-permute-start(bf16[128,1280]{1,0:T(8,128)(2,1)} %get-tuple-element.57), channel_id=1, source_target_pairs={{0,15},{1,14},{2,1},{3,0},{4,3},{5,2},{6,5},{7,4},{8,7},{9,6},{10,... | collective-permute-start | bytes 983048 | tf_op jit(solution)/shard_map/ppermute | solution.py:494
  19.5 2.1 %pack.1 = (bf16[128,2560]{1,0:T(8,128)(2,1)}, bf16[128,2560]{1,0:T(8,128)(2,1)}) custom-call(bf16[1,128,2560]{2,1,0:T(8,128)(2,1)} %a.5, bf16[1,128,2560]{2,1,0:T(8,128)(2,1)} %b.1), custom_call_target="tpu_custom_call" | custom-call | flops 2000000 | bytes 5000000 | tf_op jit(solution)/shard_map/pack/pallas_call | solution.py:102
  26.7 3.1 %collective-permute-start.7 = (bf16[128,2560]{1,0:T(8,128)(2,1)}, bf16[128,2560]{1,0:T(8,128)(2,1)S(1)}, u32[]{:S(2)}, u32[]{:S(2)}) collective-permute-start(bf16[128,2560]{1,0:T(8,128)(2,1)} %constant_dynamic-update-slice_fusion.6.refs_5_), channel_id=1, source_target_pairs={{0,14},{2,0},{4,2},{6,4},{8,6},{10,8},{12,10},{14,12},{1,15},{3,1}... | collective-permute-start | bytes 1966088 | tf_op jit(solution)/shard_map/ppermute | solution.py:494
  31.9 2.7 %collective-permute-start.5 = (bf16[128,2560]{1,0:T(8,128)(2,1)S(1)}, bf16[128,2560]{1,0:T(8,128)(2,1)S(1)}, u32[]{:S(2)}, u32[]{:S(2)}) collective-permute-start(bf16[128,2560]{1,0:T(8,128)(2,1)S(1)} %constant_dynamic-update-slice_fusion.2.refs_8_), channel_id=1, source_target_pairs={{0,14},{2,0},{4,2},{6,4},{8,6},{10,8},{12,10},{14,12},{1,15},{3,1}... | collective-permute-start | bytes 1966088 | tf_op jit(solution)/shard_map/ppermute | solution.py:454
  36.3 2.9 %query.1 = (bf16[256,1280]{1,0:T(8,128)(2,1)S(1)}, bf16[256,256]{1,0:T(8,128)(2,1)S(1)}, f32[8,256]{1,0:T(8,128)S(1)}, bf16[128,5120]{1,0:T(8,128)(2,1)S(1)}) custom-call(bf16[128,5120]{1,0:T(8,128)(2,1)S(1)} %bitcast.8, bf16[128,5120]{1,0:T(8,128)(2,1)S(1)} %collective-permute-done.8.tok_other, bf16[5120,256]{1,0:T(8,128)(2,1)S(1)} %copy-done.2, ...), custom_call_target="tpu_custom_call" | custom-call | flops 838860800 | bytes 8000000 | tf_op jit(solution)/shard_map/query/pallas_call | solution.py:148
  39.3 4.9 %shard_map.95 = (f32[8,128]{1,0:T(8,128)S(1)}, f32[256,1280]{1,0:T(8,128)S(1)}, f32[256,1280]{1,0:T(8,128)S(1)}, f32[256,1280]{1,0:T(8,128)S(1)}, f32[256,1280]{...) custom-call(s32[2]{0:T(128)S(1)} %pad_add_fusion.refs_0_, f32[8,128]{1,0:T(8,128)S(1)} %broadcast_in_dim.6.refs_1_, ...), custom_call_target="tpu_custom_call" | custom-call | flops 1677721600 | bytes 8000000 | tf_op jit(solution)/shard_map/pallas_call | solution.py:381
  48.6 9.2 %collective-permute-done.2.refs_5_ = bf16[128,2560]{1,0:T(8,128)(2,1)S(1)} collective-permute-done((bf16[128,2560]{1,0:T(8,128)(2,1)S(1)}, bf16[128,2560]{1,0:T(8,128)(2,1)S(1)}, u32[]{:S(2)}, u32[]{:S(2)}) %collective-permute-start.2) | collective-permute-done | bytes 655392 | tf_op jit(solution)/shard_map/ppermute | solution.py:453
  61.6 10.2 %collective-permute-done.13.refs_6_ = bf16[128,2560]{1,0:T(8,128)(2,1)S(1)} collective-permute-done((bf16[128,2560]{1,0:T(8,128)(2,1)S(1)}, bf16[128,2560]{1,0:T(8,128)(2,1)S(1)}, u32[]{:S(2)}, u32[]{:S(2)}) %collective-permute-start.13) | collective-permute-done | bytes 655392 | tf_op jit(solution)/shard_map/ppermute | solution.py:458
  74.0 11.8 %collective-permute-done.11.refs_5_ = bf16[128,2560]{1,0:T(8,128)(2,1)S(1)} collective-permute-done((bf16[128,2560]{1,0:T(8,128)(2,1)S(1)}, bf16[128,2560]{1,0:T(8,128)(2,1)S(1)}, u32[]{:S(2)}, u32[]{:S(2)}) %collective-permute-start.11) | collective-permute-done | bytes 655392 | tf_op jit(solution)/shard_map/ppermute | solution.py:467
  86.8 2.9 %collective-permute-start.18 = (bf16[128,1792]{1,0:T(8,128)(2,1)S(1)}, bf16[128,1792]{1,0:T(8,128)(2,1)S(1)}, u32[]{:S(2)}, u32[]{:S(2)}) collective-permute-start(bf16[128,1792]{1,0:T(8,128)(2,1)S(1)} %pad_maximum_fusion.1), channel_id=1, source_target_pairs={{0,14},{2,0},{4,2},{6,4},{8,6},{10,8},{12,10},{14,12},{1,15},{3,1}... | collective-permute-start | bytes 1376264 | tf_op jit(solution)/shard_map/ppermute | solution.py:494
  89.7 2.7 %collective-permute-start.16 = (bf16[128,2560]{1,0:T(8,128)(2,1)S(1)}, bf16[128,2560]{1,0:T(8,128)(2,1)S(1)}, u32[]{:S(2)}, u32[]{:S(2)}) collective-permute-start(bf16[128,2560]{1,0:T(8,128)(2,1)S(1)} %collective-permute-done.14.refs_7_), channel_id=1, source_target_pairs={{0,14},{2,0},{4,2},{6,4},{8,6},{10,8},{12,10},{14,12},{1,15},{3,1}... | collective-permute-start | bytes 1966088 | tf_op jit(solution)/shard_map/ppermute | solution.py:494
  92.6 2.7 %collective-permute-start.20 = (bf16[128,768]{1,0:T(8,128)(2,1)S(1)}, bf16[128,768]{1,0:T(8,128)(2,1)S(1)}, u32[]{:S(2)}, u32[]{:S(2)}) collective-permute-start(bf16[128,768]{1,0:T(8,128)(2,1)S(1)} %pad_maximum_fusion.3), channel_id=1, source_target_pairs={{0,14},{2,0},{4,2},{6,4},{8,6},{10,8},{12,10},{14,12},{1,15},{3,1}... | collective-permute-start | bytes 589832 | tf_op jit(solution)/shard_map/ppermute | solution.py:494
  95.3 10.6 %collective-permute-done.15.refs_6_ = bf16[128,2560]{1,0:T(8,128)(2,1)S(1)} collective-permute-done((bf16[128,2560]{1,0:T(8,128)(2,1)S(1)}, bf16[128,2560]{1,0:T(8,128)(2,1)S(1)}, u32[]{:S(2)}, u32[]{:S(2)}) %collective-permute-start.15) | collective-permute-done | bytes 655392 | tf_op jit(solution)/shard_map/ppermute | solution.py:494
  106.0 6.7 %collective-permute-done.16.refs_7_ = bf16[128,2560]{1,0:T(8,128)(2,1)S(1)} collective-permute-done((bf16[128,2560]{1,0:T(8,128)(2,1)S(1)}, bf16[128,2560]{1,0:T(8,128)(2,1)S(1)}, u32[]{:S(2)}, u32[]{:S(2)}) %collective-permute-start.16) | collective-permute-done | bytes 655392 | tf_op jit(solution)/shard_map/ppermute | solution.py:494
  117.2 2.8 %collective-permute-done.19.refs_5_ = bf16[128,768]{1,0:T(8,128)(2,1)S(1)} collective-permute-done((bf16[128,768]{1,0:T(8,128)(2,1)S(1)}, bf16[128,768]{1,0:T(8,128)(2,1)S(1)}, u32[]{:S(2)}, u32[]{:S(2)}) %collective-permute-start.19) | collective-permute-done | bytes 196640 | tf_op jit(solution)/shard_map/ppermute | solution.py:494
  120.0 2.8 %shard_map.100 = (bf16[128,384]{1,0:T(8,128)(2,1)}, bf16[128,384]{1,0:T(8,128)(2,1)}, bf16[16,20,128]{2,1,0:T(8,128)(2,1)}) custom-call(s32[2]{0:T(128)S(1)} %pad_add_fusion.refs_0_, f32[8,128]{1,0:T(8,128)S(1)} %get-tuple-element.90.refs_1_, bf16[256,1280]{1,0:T(8,128)(2,1)S(1)} %get-tuple-element.61.refs_2_, bf16[128,1280]{1,0:T(8,128)(2,1)S(1)} %slice.27.refs_3_, ...), custom_call_target="tpu_custom_call" | custom-call | flops 503316480 | bytes 8000000 | tf_op jit(solution)/shard_map/pallas_call | solution.py:381
  122.8 12.5 %all-to-all-start = ((bf16[16,20,128]{2,1,0:T(8,128)(2,1)}), bf16[16,20,128]{2,1,0:T(8,128)(2,1)S(1)}, u32[]{:S(2)}, u32[]{:S(2)}) async-start(bf16[16,20,128]{2,1,0:T(8,128)(2,1)} %get-tuple-element.107), calls=%async_computation | async-start | bytes 196608 | tf_op jit(solution)/shard_map/all_to_all | solution.py:400
  135.9 7.9 %all-to-all-done = bf16[16,20,128]{2,1,0:T(8,128)(2,1)S(1)} async-done(((bf16[16,20,128]{2,1,0:T(8,128)(2,1)}), bf16[16,20,128]{2,1,0:T(8,128)(2,1)S(1)}, u32[]{:S(2)}, u32[]{:S(2)}) %all-to-all-start) | async-done | bytes 81952 | tf_op jit(solution)/shard_map/all_to_all | solution.py:400
  144.4 6.7 %all-to-all-start.1 = ((bf16[16,20,128]{2,1,0:T(8,128)(2,1)}), bf16[16,20,128]{2,1,0:T(8,128)(2,1)S(1)}, u32[]{:S(2)}, u32[]{:S(2)}) async-start(bf16[16,20,128]{2,1,0:T(8,128)(2,1)} %broadcast_in_dim.7), calls=%async_computation.1 | async-start | bytes 196608 | tf_op jit(solution)/shard_map/all_to_all | solution.py:396
  151.2 6.6 %all-to-all-done.1 = bf16[16,20,128]{2,1,0:T(8,128)(2,1)S(1)} async-done(((bf16[16,20,128]{2,1,0:T(8,128)(2,1)}), bf16[16,20,128]{2,1,0:T(8,128)(2,1)S(1)}, u32[]{:S(2)}, u32[]{:S(2)}) %all-to-all-start.1) | async-done | bytes 81952 | tf_op jit(solution)/shard_map/all_to_all | solution.py:396
  158.4 4.7 %all-to-all-start.2 = ((bf16[16,20,128]{2,1,0:T(8,128)(2,1)}), bf16[16,20,128]{2,1,0:T(8,128)(2,1)S(1)}, u32[]{:S(2)}, u32[]{:S(2)}) async-start(bf16[16,20,128]{2,1,0:T(8,128)(2,1)} %broadcast_in_dim.8), calls=%async_computation.2 | async-start | bytes 196608 | tf_op jit(solution)/shard_map/all_to_all | solution.py:396
  163.1 2.0 %maximum_select_fusion = bf16[1,128,2560]{2,1,0:T(8,128)(2,1)} fusion(bf16[1,128,384]{2,1,0:T(8,128)(2,1)S(1)} %bitcast.13, bf16[1,128,896]{2,1,0:T(8,128)(2,1)S(1)} %bitcast.11, bf16[1,128,384]{2,1,0:T(8,128)(2,1)} %bitcast.12, bf16[1,128,896]{2,1,0:T(8,128)(2,1)S(1)} %bitcast.10, pred[]{:T(512)S(6)} %eq.3), kind=kLoop, calls=%fused_computation | loop fusion | flops 5570560 | bytes 1310721 | tf_op jit(solution)/shard_map/jit(_where)/select_n | solution.py:485
  165.1 6.5 %all-to-all-done.2.blocks = bf16[16,20,128]{2,1,0:T(8,128)(2,1)S(1)} async-done(((bf16[16,20,128]{2,1,0:T(8,128)(2,1)}), bf16[16,20,128]{2,1,0:T(8,128)(2,1)S(1)}, u32[]{:S(2)}, u32[]{:S(2)}) %all-to-all-start.2) | async-done | bytes 81952 | tf_op jit(solution)/shard_map/all_to_all | solution.py:396
  (78 shorter events, 40.7 us)
Async XLA Ops:
  0.6 31.2 %collective-permute-start.8 = (bf16[128,5120]{1,0:T(8,128)(2,1)}, bf16[128,5120]{1,0:T(8,128)(2,1)S(1)}, u32[]{:S(2)}, u32[]{:S(2)}) collective-permute-start(bf16[128,5120]{1,0:T(8,128)(2,1)} %bitcast.7), channel_id=1, source_target_pairs={{0,1},{1,0},{2,3},{3,2},{4,5},{5,4},{6,7},{7,6},{8,9},{9,8},{10,11... | collective-permute-start | bytes 3932168 | tf_op jit(solution)/shard_map/ppermute | solution.py:494
  5.8 16.9 %collective-permute-start = (bf16[128,1280]{1,0:T(8,128)(2,1)}, bf16[128,1280]{1,0:T(8,128)(2,1)}, u32[]{:S(2)}, u32[]{:S(2)}) collective-permute-start(bf16[128,1280]{1,0:T(8,128)(2,1)} %get-tuple-element.55), channel_id=1, source_target_pairs={{0,2},{2,4},{4,6},{6,8},{8,10},{10,12},{12,14},{14,0},{1,3},{3,5},... | collective-permute-start | bytes 983048 | tf_op jit(solution)/shard_map/ppermute | solution.py:494
  7.7 17.8 %collective-permute-start.1 = (bf16[128,1280]{1,0:T(8,128)(2,1)}, bf16[128,1280]{1,0:T(8,128)(2,1)}, u32[]{:S(2)}, u32[]{:S(2)}) collective-permute-start(bf16[128,1280]{1,0:T(8,128)(2,1)} %get-tuple-element.56), channel_id=1, source_target_pairs={{0,2},{2,4},{4,6},{6,8},{8,10},{10,12},{12,14},{14,0},{1,3},{3,5},... | collective-permute-start | bytes 983048 | tf_op jit(solution)/shard_map/ppermute | solution.py:494
  9.3 14.9 %collective-permute-start.3 = (bf16[128,1280]{1,0:T(8,128)(2,1)}, bf16[128,1280]{1,0:T(8,128)(2,1)}, u32[]{:S(2)}, u32[]{:S(2)}) collective-permute-start(bf16[128,1280]{1,0:T(8,128)(2,1)} %get-tuple-element.57), channel_id=1, source_target_pairs={{0,15},{1,14},{2,1},{3,0},{4,3},{5,2},{6,5},{7,4},{8,7},{9,6},{10,... | collective-permute-start | bytes 983048 | tf_op jit(solution)/shard_map/ppermute | solution.py:494
  11.8 14.9 %collective-permute-start.4 = (bf16[128,1280]{1,0:T(8,128)(2,1)}, bf16[128,1280]{1,0:T(8,128)(2,1)}, u32[]{:S(2)}, u32[]{:S(2)}) collective-permute-start(bf16[128,1280]{1,0:T(8,128)(2,1)} %get-tuple-element.58), channel_id=1, source_target_pairs={{0,15},{1,14},{2,1},{3,0},{4,3},{5,2},{6,5},{7,4},{8,7},{9,6},{10,... | collective-permute-start | bytes 983048 | tf_op jit(solution)/shard_map/ppermute | solution.py:494
  24.3 15.0 %collective-permute-start.10 = (bf16[128,2560]{1,0:T(8,128)(2,1)}, bf16[128,2560]{1,0:T(8,128)(2,1)S(1)}, u32[]{:S(2)}, u32[]{:S(2)}) collective-permute-start(bf16[128,2560]{1,0:T(8,128)(2,1)} %constant_dynamic-update-slice_fusion.4), channel_id=1, source_target_pairs={{0,1},{1,0},{2,3},{3,2},{4,5},{5,4},{6,7},{7,6},{8,9},{9,8},{10,11... | collective-permute-start | bytes 1966088 | tf_op jit(solution)/shard_map/ppermute | solution.py:494
  25.5 18.7 %collective-permute-start.6 = (bf16[128,2560]{1,0:T(8,128)(2,1)}, bf16[128,2560]{1,0:T(8,128)(2,1)S(1)}, u32[]{:S(2)}, u32[]{:S(2)}) collective-permute-start(bf16[128,2560]{1,0:T(8,128)(2,1)} %constant_dynamic-update-slice_fusion.4), channel_id=1, source_target_pairs={{0,3},{1,2},{2,5},{3,4},{4,7},{5,6},{6,9},{7,8},{8,11},{9,10},{10,... | collective-permute-start | bytes 1966088 | tf_op jit(solution)/shard_map/ppermute | solution.py:494
  26.7 18.2 %collective-permute-start.7 = (bf16[128,2560]{1,0:T(8,128)(2,1)}, bf16[128,2560]{1,0:T(8,128)(2,1)S(1)}, u32[]{:S(2)}, u32[]{:S(2)}) collective-permute-start(bf16[128,2560]{1,0:T(8,128)(2,1)} %constant_dynamic-update-slice_fusion.6.refs_5_), channel_id=1, source_target_pairs={{0,14},{2,0},{4,2},{6,4},{8,6},{10,8},{12,10},{14,12},{1,15},{3,1}... | collective-permute-start | bytes 1966088 | tf_op jit(solution)/shard_map/ppermute | solution.py:494
  31.7 26.0 %collective-permute-start.2 = (bf16[128,2560]{1,0:T(8,128)(2,1)S(1)}, bf16[128,2560]{1,0:T(8,128)(2,1)S(1)}, u32[]{:S(2)}, u32[]{:S(2)}) collective-permute-start(bf16[128,2560]{1,0:T(8,128)(2,1)S(1)} %constant_dynamic-update-slice_fusion.refs_5_), channel_id=1, source_target_pairs={{0,2},{2,4},{4,6},{6,8},{8,10},{10,12},{12,14},{14,0},{1,3},{3,5},... | collective-permute-start | bytes 1966088 | tf_op jit(solution)/shard_map/ppermute | solution.py:453
  31.9 27.0 %collective-permute-start.5 = (bf16[128,2560]{1,0:T(8,128)(2,1)S(1)}, bf16[128,2560]{1,0:T(8,128)(2,1)S(1)}, u32[]{:S(2)}, u32[]{:S(2)}) collective-permute-start(bf16[128,2560]{1,0:T(8,128)(2,1)S(1)} %constant_dynamic-update-slice_fusion.2.refs_8_), channel_id=1, source_target_pairs={{0,14},{2,0},{4,2},{6,4},{8,6},{10,8},{12,10},{14,12},{1,15},{3,1}... | collective-permute-start | bytes 1966088 | tf_op jit(solution)/shard_map/ppermute | solution.py:454
  44.8 26.9 %collective-permute-start.13 = (bf16[128,2560]{1,0:T(8,128)(2,1)S(1)}, bf16[128,2560]{1,0:T(8,128)(2,1)S(1)}, u32[]{:S(2)}, u32[]{:S(2)}) collective-permute-start(bf16[128,2560]{1,0:T(8,128)(2,1)S(1)} %collective-permute-done.6.refs_6_), channel_id=1, source_target_pairs={{0,2},{2,4},{4,6},{6,8},{8,10},{10,12},{12,14},{14,0},{1,3},{3,5},... | collective-permute-start | bytes 1966088 | tf_op jit(solution)/shard_map/ppermute | solution.py:458
  46.4 26.6 %collective-permute-start.14 = (bf16[128,2560]{1,0:T(8,128)(2,1)S(1)}, bf16[128,2560]{1,0:T(8,128)(2,1)S(1)}, u32[]{:S(2)}, u32[]{:S(2)}) collective-permute-start(bf16[128,2560]{1,0:T(8,128)(2,1)S(1)} %collective-permute-done.7.refs_7_), channel_id=1, source_target_pairs={{0,14},{2,0},{4,2},{6,4},{8,6},{10,8},{12,10},{14,12},{1,15},{3,1}... | collective-permute-start | bytes 1966088 | tf_op jit(solution)/shard_map/ppermute | solution.py:459
  58.9 26.9 %collective-permute-start.11 = (bf16[128,2560]{1,0:T(8,128)(2,1)S(1)}, bf16[128,2560]{1,0:T(8,128)(2,1)S(1)}, u32[]{:S(2)}, u32[]{:S(2)}) collective-permute-start(bf16[128,2560]{1,0:T(8,128)(2,1)S(1)} %collective-permute-done.2.refs_5_), channel_id=1, source_target_pairs={{0,2},{2,4},{4,6},{6,8},{8,10},{10,12},{12,14},{14,0},{1,3},{3,5},... | collective-permute-start | bytes 1966088 | tf_op jit(solution)/shard_map/ppermute | solution.py:467
  60.4 26.2 %collective-permute-start.12 = (bf16[128,2560]{1,0:T(8,128)(2,1)S(1)}, bf16[128,2560]{1,0:T(8,128)(2,1)S(1)}, u32[]{:S(2)}, u32[]{:S(2)}) collective-permute-start(bf16[128,2560]{1,0:T(8,128)(2,1)S(1)} %collective-permute-done.5.refs_8_), channel_id=1, source_target_pairs={{0,14},{2,0},{4,2},{6,4},{8,6},{10,8},{12,10},{14,12},{1,15},{3,1}... | collective-permute-start | bytes 1966088 | tf_op jit(solution)/shard_map/ppermute | solution.py:468
  86.8 27.2 %collective-permute-start.18 = (bf16[128,1792]{1,0:T(8,128)(2,1)S(1)}, bf16[128,1792]{1,0:T(8,128)(2,1)S(1)}, u32[]{:S(2)}, u32[]{:S(2)}) collective-permute-start(bf16[128,1792]{1,0:T(8,128)(2,1)S(1)} %pad_maximum_fusion.1), channel_id=1, source_target_pairs={{0,14},{2,0},{4,2},{6,4},{8,6},{10,8},{12,10},{14,12},{1,15},{3,1}... | collective-permute-start | bytes 1376264 | tf_op jit(solution)/shard_map/ppermute | solution.py:494
  89.7 16.3 %collective-permute-start.15 = (bf16[128,2560]{1,0:T(8,128)(2,1)S(1)}, bf16[128,2560]{1,0:T(8,128)(2,1)S(1)}, u32[]{:S(2)}, u32[]{:S(2)}) collective-permute-start(bf16[128,2560]{1,0:T(8,128)(2,1)S(1)} %collective-permute-done.13.refs_6_), channel_id=1, source_target_pairs={{0,2},{2,4},{4,6},{6,8},{8,10},{10,12},{12,14},{14,0},{1,3},{3,5},... | collective-permute-start | bytes 1966088 | tf_op jit(solution)/shard_map/ppermute | solution.py:494
  89.7 23.0 %collective-permute-start.16 = (bf16[128,2560]{1,0:T(8,128)(2,1)S(1)}, bf16[128,2560]{1,0:T(8,128)(2,1)S(1)}, u32[]{:S(2)}, u32[]{:S(2)}) collective-permute-start(bf16[128,2560]{1,0:T(8,128)(2,1)S(1)} %collective-permute-done.14.refs_7_), channel_id=1, source_target_pairs={{0,14},{2,0},{4,2},{6,4},{8,6},{10,8},{12,10},{14,12},{1,15},{3,1}... | collective-permute-start | bytes 1966088 | tf_op jit(solution)/shard_map/ppermute | solution.py:494
  92.4 23.4 %collective-permute-start.17 = (bf16[128,1792]{1,0:T(8,128)(2,1)S(1)}, bf16[128,1792]{1,0:T(8,128)(2,1)S(1)}, u32[]{:S(2)}, u32[]{:S(2)}) collective-permute-start(bf16[128,1792]{1,0:T(8,128)(2,1)S(1)} %pad_maximum_fusion), channel_id=1, source_target_pairs={{0,2},{2,4},{4,6},{6,8},{8,10},{10,12},{12,14},{14,0},{1,3},{3,5},... | collective-permute-start | bytes 1376264 | tf_op jit(solution)/shard_map/ppermute | solution.py:494
  92.6 24.6 %collective-permute-start.20 = (bf16[128,768]{1,0:T(8,128)(2,1)S(1)}, bf16[128,768]{1,0:T(8,128)(2,1)S(1)}, u32[]{:S(2)}, u32[]{:S(2)}) collective-permute-start(bf16[128,768]{1,0:T(8,128)(2,1)S(1)} %pad_maximum_fusion.3), channel_id=1, source_target_pairs={{0,14},{2,0},{4,2},{6,4},{8,6},{10,8},{12,10},{14,12},{1,15},{3,1}... | collective-permute-start | bytes 589832 | tf_op jit(solution)/shard_map/ppermute | solution.py:494
  106.0 14.0 %collective-permute-start.19 = (bf16[128,768]{1,0:T(8,128)(2,1)S(1)}, bf16[128,768]{1,0:T(8,128)(2,1)S(1)}, u32[]{:S(2)}, u32[]{:S(2)}) collective-permute-start(bf16[128,768]{1,0:T(8,128)(2,1)S(1)} %pad_maximum_fusion.2), channel_id=1, source_target_pairs={{0,2},{2,4},{4,6},{6,8},{8,10},{10,12},{12,14},{14,0},{1,3},{3,5},... | collective-permute-start | bytes 589832 | tf_op jit(solution)/shard_map/ppermute | solution.py:494
  122.8 21.0 %all-to-all-start = ((bf16[16,20,128]{2,1,0:T(8,128)(2,1)}), bf16[16,20,128]{2,1,0:T(8,128)(2,1)S(1)}, u32[]{:S(2)}, u32[]{:S(2)}) async-start(bf16[16,20,128]{2,1,0:T(8,128)(2,1)} %get-tuple-element.107), calls=%async_computation | async-start | bytes 196608 | tf_op jit(solution)/shard_map/all_to_all | solution.py:400
  135.3 27.8 %collective-permute-start.21 = (bf16[128,896]{1,0:T(8,128)(2,1)S(1)}, bf16[128,896]{1,0:T(8,128)(2,1)S(1)}, u32[]{:S(2)}, u32[]{:S(2)}) collective-permute-start(bf16[128,896]{1,0:T(8,128)(2,1)S(1)} %copy-done.7), channel_id=1, source_target_pairs={{0,1},{1,0},{2,3},{3,2},{4,5},{5,4},{6,7},{7,6},{8,9},{9,8},{10,11... | collective-permute-start | bytes 688136 | tf_op jit(solution)/shard_map/ppermute | solution.py:484
  135.5 27.6 %collective-permute-start.22 = (bf16[128,384]{1,0:T(8,128)(2,1)}, bf16[128,384]{1,0:T(8,128)(2,1)S(1)}, u32[]{:S(2)}, u32[]{:S(2)}) collective-permute-start(bf16[128,384]{1,0:T(8,128)(2,1)} %get-tuple-element.106), channel_id=1, source_target_pairs={{0,1},{1,0},{2,3},{3,2},{4,5},{5,4},{6,7},{7,6},{8,9},{9,8},{10,11... | collective-permute-start | bytes 294920 | tf_op jit(solution)/shard_map/ppermute | solution.py:484
  144.4 13.3 %all-to-all-start.1 = ((bf16[16,20,128]{2,1,0:T(8,128)(2,1)}), bf16[16,20,128]{2,1,0:T(8,128)(2,1)S(1)}, u32[]{:S(2)}, u32[]{:S(2)}) async-start(bf16[16,20,128]{2,1,0:T(8,128)(2,1)} %broadcast_in_dim.7), calls=%async_computation.1 | async-start | bytes 196608 | tf_op jit(solution)/shard_map/all_to_all | solution.py:396
  (10 other events, 143.0 us)
